TPU v7x, 16 devices: a whole 2x2x2 slice. The times are simulated.
16 devices in a mesh: tp: 2 (over z), dp: 8 (over y, x, core).
Axes of the slice: x: 2, y: 2, z: 2, core: 2. Of those that a mesh axis runs over, the one named last changes fastest.
Arguments:
- token_ids: int32 [256, 256], P('dp')
- embed_table: bfloat16 [50304, 1024], P('tp')
- ln1_gain: bfloat16 [1024], replicated
- ln1_bias: bfloat16 [1024], replicated
- ln2_gain: bfloat16 [1024], replicated
- ln2_bias: bfloat16 [1024], replicated
- w_qkv: bfloat16 [1024, 16, 3, 64], P(None, 'tp')
- b_qkv: bfloat16 [16, 3, 64], P('tp')
- w_dense: bfloat16 [16, 64, 1024], P('tp')
- b_dense: bfloat16 [1024], replicated
- w_fc1: bfloat16 [1024, 4096], P(None, 'tp')
- b_fc1: bfloat16 [4096], P('tp')
- w_fc2: bfloat16 [4096, 1024], P('tp')
- b_fc2: bfloat16 [1024], replicated
- cotangent: bfloat16 [256, 256, 1024], P('dp')
Outputs:
- output 1: bfloat16 [256, 256, 1024], P('dp')
- output 2: float32 [50304, 1024], P('tp', 'dp')
- output 3: float32 [1024], P('dp')
- output 4: float32 [1024], P('dp')
- output 5: float32 [1024], P('dp')
- output 6: float32 [1024], P('dp')
- output 7: float32 [1024, 16, 3, 64], P('dp', 'tp')
- output 8: float32 [3072], P(('tp', 'dp'))
- output 9: float32 [16, 64, 1024], P('tp', None, 'dp')
- output 10: float32 [1024], P('dp')
- output 11: float32 [1024, 4096], P('dp', 'tp')
- output 12: float32 [4096], P(('tp', 'dp'))
- output 13: float32 [4096, 1024], P('tp', 'dp')
- output 14: float32 [1024], P('dp')
All inputs are finite; a program needn't handle non-finite values.
Results may differ from a plain program's by a relative error of at most 0.0100979.
Values sent between devices are 32-bit elements.
A program may use at most 1 GiB of HBM per device.

v0:
```python
import functools
import jax
import jax.numpy as jnp
from jax import lax
from jax.sharding import PartitionSpec as P

EPS_NORM = 1e-5
ROPE_BASE = 10000.0
gelu_exact = functools.partial(jax.nn.gelu, approximate=False)


def rope_tables(seq_len, rot_dim):
    half_rot = rot_dim // 2
    inv_freq = ROPE_BASE ** (-(jnp.arange(half_rot, dtype=jnp.float32) * 2.0) / rot_dim)
    angles = jnp.arange(seq_len, dtype=jnp.float32)[:, None] * inv_freq[None, :]
    angles = jnp.concatenate([angles, angles], axis=-1)
    return jnp.cos(angles)[:, None, :], jnp.sin(angles)[:, None, :]


def apply_rope(tensor, cos_table, sin_table, rot_dim):
    half_rot = rot_dim // 2
    rot_part = tensor[..., :rot_dim]
    turned = jnp.concatenate([-rot_part[..., half_rot:], rot_part[..., :half_rot]], axis=-1)
    return jnp.concatenate([rot_part * cos_table + turned * sin_table, tensor[..., rot_dim:]], axis=-1)


def rope_back(grad_in, cos_table, sin_table, rot_dim):
    half_rot = rot_dim // 2
    rot_part = grad_in[..., :rot_dim]
    spun_part = rot_part * sin_table
    turned = jnp.concatenate([spun_part[..., half_rot:], -spun_part[..., :half_rot]], axis=-1)
    return jnp.concatenate([rot_part * cos_table + turned, grad_in[..., rot_dim:]], axis=-1)


def solution(mesh):
    arg_specs = (P('dp', None), P('tp', None), P(None), P(None), P(None), P(None), P(None, 'tp', None, None), P('tp', None, None), P('tp', None, None), P(None), P(None, 'tp'), P('tp'), P('tp', None), P(None), P('dp', None, None))
    out_specs = (P('dp', None, None), P('tp', 'dp'), P('dp'), P('dp'), P('dp'), P('dp'), P('dp', 'tp', None, None), P(('tp', 'dp')), P('tp', None, 'dp'), P('dp'), P('dp', 'tp'), P(('tp', 'dp')), P('tp', 'dp'), P('dp'))

    def device_step(token_ids, embed_table, ln1_gain, ln1_bias, ln2_gain, ln2_bias, w_qkv, b_qkv, w_dense, b_dense, w_fc1, b_fc1, w_fc2, b_fc2, cotangent):
        seq_len = token_ids.shape[1]
        vocab_local, d_model = embed_table.shape
        head_dim = w_qkv.shape[3]
        rot_dim = head_dim // 4
        attn_scale = head_dim ** -0.5
        local_ids = token_ids - lax.axis_index('tp') * vocab_local
        in_range = (local_ids >= 0) & (local_ids < vocab_local)
        picked = jnp.take(embed_table, jnp.where(in_range, local_ids, 0), axis=0)
        partial_x = jnp.where(in_range[..., None], picked, jnp.zeros_like(picked))
        x_float = lax.psum(partial_x.astype(jnp.float32), 'tp')
        mean_x = jnp.mean(x_float, axis=-1, keepdims=True)
        centered = x_float - mean_x
        inv_std = lax.rsqrt(jnp.mean(centered * centered, axis=-1, keepdims=True) + EPS_NORM)
        normed = centered * inv_std
        gain_attn = ln1_gain.astype(jnp.float32)
        gain_mlp = ln2_gain.astype(jnp.float32)
        hid_attn = (normed * gain_attn + ln1_bias.astype(jnp.float32)).astype(jnp.bfloat16)
        hid_mlp = (normed * gain_mlp + ln2_bias.astype(jnp.float32)).astype(jnp.bfloat16)
        qkv_all = (jnp.einsum('bsd,dhjc->bshjc', hid_attn, w_qkv, preferred_element_type=jnp.float32) + b_qkv.astype(jnp.float32)).astype(jnp.bfloat16)
        cos_table, sin_table = rope_tables(seq_len, rot_dim)
        queries = apply_rope(qkv_all[:, :, :, 0].astype(jnp.float32), cos_table, sin_table, rot_dim).astype(jnp.bfloat16)
        keys_rot = apply_rope(qkv_all[:, :, :, 1].astype(jnp.float32), cos_table, sin_table, rot_dim).astype(jnp.bfloat16)
        values = qkv_all[:, :, :, 2]
        causal = jnp.arange(seq_len)[:, None] >= jnp.arange(seq_len)[None, :]
        scores = jnp.einsum('bqhc,bkhc->bhqk', queries, keys_rot, preferred_element_type=jnp.float32) * attn_scale
        soft_probs = jax.nn.softmax(jnp.where(causal, scores, -1e30), axis=-1)
        probs_low = soft_probs.astype(jnp.bfloat16)
        context = jnp.einsum('bhqk,bkhc->bqhc', probs_low, values, preferred_element_type=jnp.float32).astype(jnp.bfloat16)
        pre_act = (jnp.einsum('bsd,df->bsf', hid_mlp, w_fc1, preferred_element_type=jnp.float32) + b_fc1.astype(jnp.float32)).astype(jnp.bfloat16)
        act_float, gelu_pull = jax.vjp(gelu_exact, pre_act.astype(jnp.float32))
        gelu_out = act_float.astype(jnp.bfloat16)
        partial_out = jnp.einsum('crid,ide->cre', context, w_dense, preferred_element_type=jnp.float32) + jnp.einsum('bsf,fd->bsd', gelu_out, w_fc2, preferred_element_type=jnp.float32)
        layer_sum = lax.psum(partial_out, 'tp')
        layer_out = (x_float + layer_sum + (b_dense.astype(jnp.float32) + b_fc2.astype(jnp.float32))).astype(jnp.bfloat16)

        cot_float = cotangent.astype(jnp.float32)
        bias_grad = jnp.sum(cot_float, axis=(0, 1))
        grad_act = jnp.einsum('bsd,fd->bsf', cotangent, w_fc2, preferred_element_type=jnp.float32).astype(jnp.bfloat16)
        (grad_pre_float,) = gelu_pull(grad_act.astype(jnp.float32))
        grad_pre = grad_pre_float.astype(jnp.bfloat16)
        part_wfc2 = jnp.einsum('bsf,bsd->fd', gelu_out, cotangent, preferred_element_type=jnp.float32)
        part_wfc1 = jnp.einsum('bsd,bsf->df', hid_mlp, grad_pre, preferred_element_type=jnp.float32)
        part_bfc1 = jnp.sum(grad_pre.astype(jnp.float32), axis=(0, 1))
        grad_hmlp = jnp.einsum('bsf,df->bsd', grad_pre, w_fc1, preferred_element_type=jnp.float32)
        part_wdense = jnp.einsum('crid,cre->ide', context, cotangent, preferred_element_type=jnp.float32)
        grad_ctx = jnp.einsum('cre,ide->crid', cotangent, w_dense, preferred_element_type=jnp.float32).astype(jnp.bfloat16)
        grad_probs = jnp.einsum('bqhc,bkhc->bhqk', grad_ctx, values, preferred_element_type=jnp.float32).astype(jnp.bfloat16).astype(jnp.float32)
        grad_values = jnp.einsum('bhqk,bqhc->bkhc', probs_low, grad_ctx, preferred_element_type=jnp.float32)
        grad_scores = (soft_probs * (grad_probs - jnp.sum(soft_probs * grad_probs, axis=-1, keepdims=True)) * attn_scale).astype(jnp.bfloat16)
        grad_queries = jnp.einsum('bhqk,bkhc->bqhc', grad_scores, keys_rot, preferred_element_type=jnp.float32).astype(jnp.bfloat16).astype(jnp.float32)
        grad_keys = jnp.einsum('bhqk,bqhc->bkhc', grad_scores, queries, preferred_element_type=jnp.float32).astype(jnp.bfloat16).astype(jnp.float32)
        grad_qkv = jnp.stack([rope_back(grad_queries, cos_table, sin_table, rot_dim), rope_back(grad_keys, cos_table, sin_table, rot_dim), grad_values], axis=3).astype(jnp.bfloat16)
        part_wqkv = jnp.einsum('bsd,bshjc->dhjc', hid_attn, grad_qkv, preferred_element_type=jnp.float32)
        part_bqkv = jnp.sum(grad_qkv.astype(jnp.float32), axis=(0, 1))
        grad_hattn = jnp.einsum('bshjc,dhjc->bsd', grad_qkv, w_qkv, preferred_element_type=jnp.float32)
        ln_parts = jnp.stack([jnp.sum(grad_hattn * normed, axis=(0, 1)), jnp.sum(grad_hattn, axis=(0, 1)), jnp.sum(grad_hmlp * normed, axis=(0, 1)), jnp.sum(grad_hmlp, axis=(0, 1))])
        grad_norm_part = grad_hattn * gain_attn + grad_hmlp * gain_mlp
        grad_norm = lax.psum(grad_norm_part, 'tp')
        grad_x = cot_float + inv_std * (grad_norm - jnp.mean(grad_norm, axis=-1, keepdims=True) - normed * jnp.mean(grad_norm * normed, axis=-1, keepdims=True))
        seg_ids = jnp.where(in_range, local_ids, vocab_local).reshape(-1)
        embed_part = jax.ops.segment_sum(grad_x.reshape(-1, d_model), seg_ids, num_segments=vocab_local, mode='drop')

        sum_embed = lax.psum_scatter(embed_part, 'dp', scatter_dimension=1, tiled=True)
        sum_ln = lax.psum(lax.psum_scatter(ln_parts, 'dp', scatter_dimension=1, tiled=True), 'tp')
        sum_wqkv = lax.psum_scatter(part_wqkv, 'dp', scatter_dimension=0, tiled=True)
        sum_bqkv = lax.psum_scatter(part_bqkv.reshape(-1), 'dp', scatter_dimension=0, tiled=True)
        sum_wdense = lax.psum_scatter(part_wdense, 'dp', scatter_dimension=2, tiled=True)
        sum_bias = lax.psum_scatter(bias_grad, 'dp', scatter_dimension=0, tiled=True)
        sum_wfc1 = lax.psum_scatter(part_wfc1, 'dp', scatter_dimension=0, tiled=True)
        sum_bfc1 = lax.psum_scatter(part_bfc1, 'dp', scatter_dimension=0, tiled=True)
        sum_wfc2 = lax.psum_scatter(part_wfc2, 'dp', scatter_dimension=1, tiled=True)
        return (layer_out, sum_embed, sum_ln[0], sum_ln[1], sum_ln[2], sum_ln[3], sum_wqkv, sum_bqkv, sum_wdense, sum_bias, sum_wfc1, sum_bfc1, sum_wfc2, sum_bias)

    return jax.shard_map(device_step, mesh=mesh, in_specs=arg_specs, out_specs=out_specs, check_vma=False)
```

profile of v0, /device:TPU:0, one launch (start us, length us, event | category | flops | bytes accessed | tf_op | source)
XLA Modules:
  0.0 4456.9 jit_solution(13330209541134892153)
XLA Ops:
  8.2 1.4 select_bitcast_fusion
  9.6 157.5 %gather_fusion = bf16[8192,1024]{1,0:T(8,128)(2,1)} fusion(bf16[25152,1024]{1,0:T(8,128)(2,1)} %param.16, s32[8192]{0:T(1024)S(1)} %broadcast_clamp_fusion.1), kind=kCustom, calls=%fused_computation | custom fusion | bytes 33587200 | tf_op jit(solution)/shard_map/jit(_take)/gather | solution.py:47
  167.1 18.6 select_convert_fusion
  188.5 14.7 fusion.80
  203.1 957.1 %all-reduce.8.cloned.1.call-done = f32[32,256,1024]{2,1,0:T(8,128)} async-done(((f32[32,256,1024]{2,1,0:T(8,128)}), f32[32,256,1024]{2,1,0:T(8,128)}) %all-reduce.8.cloned.1.call-update) | async-done | bytes 33554448 | tf_op jit(solution)/shard_map/psum | solution.py:49
  1160.2 11.8 reduce_sum.117
  1172.1 13.0 multiply_reduce_fusion.2
  1185.2 34.3 add_convert_fusion.1
  1219.5 21.3 fusion.127
  1240.8 20.8 convolution_convert_fusion
  1261.6 6.1 slice.122
  1267.7 6.1 slice.117
  1273.8 4.4 slice_negate_fusion.2
  1278.3 5.7 fusion.90
  1284.0 32.4 fusion.133
  1316.4 27.7 fusion.75
  1344.0 89.4 %convert_bitcast_fusion.2 = bf16[32,256,8,64]{1,3,2,0:T(8,128)(2,1)} fusion(bf16[32,8,256,256]{2,3,1,0:T(8,128)(2,1)} %convolution_convert_fusion, bf16[32,256,8,48]{1,3,2,0:T(8,128)(2,1)} %slice.122, bf16[32,256,8,16]{1,3,2,0:T(8,128)(2,1)} %get-tuple-element.47, f32[32,8,256,256]{2,3,1,0:T(8,128)} %get-tuple-element.61, ...), kind=kOutput, calls=%fused_computation.113 | convolution fusion | flops 2319515904 | bytes 117702656 | tf_op jit(solution)/shard_map/bhqk,bkhc->bqhc/dot_general | solution.py:89
  1433.4 68.5 %convert_bitcast_fusion.1 = bf16[32,256,8,64]{1,3,2,0:T(8,128)(2,1)} fusion(bf16[32,8,256,256]{2,3,1,0:T(8,128)(2,1)} %convolution_convert_fusion, bf16[32,256,8,48]{1,3,2,0:T(8,128)(2,1)} %slice.117, bf16[32,256,8,16]{1,3,2,0:T(8,128)(2,1)} %get-tuple-element.46, f32[32,8,256,256]{2,3,1,0:T(8,128)} %get-tuple-element.61, ...), kind=kOutput, calls=%fused_computation.112 | convolution fusion | flops 2319515904 | bytes 117702656 | tf_op jit(solution)/shard_map/bhqk,bqhc->bkhc/dot_general | solution.py:90
  1501.9 28.2 convert_bitcast_fusion
  1530.1 6.2 slice.130
  1536.3 6.1 slice.126
  1542.4 3.5 convert_multiply_fusion.17
  1545.9 2.6 fusion.131
  1548.5 2.6 fusion.132
  1551.1 18.9 fusion.73
  1570.1 178.2 %fusion.33 = (f32[32,256,2048]{2,1,0:T(8,128)}, bf16[32,256,2048]{2,1,0:T(8,128)(2,1)}) fusion(f32[2048]{0:T(1024)S(1)} %copy-done.24, bf16[1024,2048]{1,0:T(8,128)(2,1)S(1)} %copy-done.39, f32[1024]{0:T(1024)S(1)} %copy-done.31, f32[1024]{0:T(1024)S(1)} %copy-done.28, f32[32,256]{1,0:T(8,128)S(1)} %copy-done.9, ...), kind=kOutput, calls=%fused_computation.42 | convolution fusion | flops 35492200448 | bytes 138493952 | tf_op jit(solution)/shard_map/bsd,df->bsf/dot_general | solution.py:68
  1748.3 65.9 %convert_reduce_fusion = (f32[2048]{0:T(1024)}, bf16[32,256,2048]{2,1,0:T(8,128)(2,1)}) fusion(f32[32,256,2048]{2,1,0:T(8,128)} %get-tuple-element.62, bf16[32,256,1024]{2,1,0:T(8,128)(2,1)} %param.29, bf16[2048,1024]{1,0:T(8,128)(2,1)} %param.27, bf16[32,256,2048]{2,1,0:T(8,128)(2,1)} %get-tuple-element.63), kind=kOutput, calls=%fused_computation.53 | convolution fusion | flops 34678505472 | bytes 155197440 | tf_op jit(solution)/shard_map/bsd,fd->bsf/dot_general | solution.py:77
  1814.2 58.3 %bitcast_add_fusion = f32[32,256,1024]{2,1,0:T(8,128)} fusion(f32[32,256,1024,1]{2,1,3,0:T(8,128)} %fusion.73, bf16[2048,1024]{1,0:T(8,128)(2,1)} %param.27, f32[32,256,2048]{2,1,0:T(8,128)} %get-tuple-element.62, bf16[32,256,2048]{2,1,0:T(8,128)(2,1)} %get-tuple-element.63), kind=kOutput, calls=%fused_computation.71 | convolution fusion | flops 34435235840 | bytes 171966464 | tf_op jit(solution)/shard_map/bsf,fd->bsd/dot_general | solution.py:71
  1872.6 42.1 fusion.93
  1914.7 4.8 fusion.84
  1919.5 8.2 maximum_bitcast_fusion
  1927.7 8.3 maximum_bitcast_fusion.1
  1936.0 22.3 convert_reduce_fusion.1
  1958.3 48.7 %fusion.51 = (f32[32,256,1024]{2,1,0:T(8,128)}, f32[32,256,1024,1,1]{2,1,3,0,4:T(8,128)}) fusion(f32[32,256,1024]{2,1,0:T(8,128)} %fusion.93, f32[1024]{0:T(1024)S(1)} %copy-done.29, f32[1024]{0:T(1024)S(1)} %copy-done.21, bf16[32,256,8,3,64]{1,4,2,0,3:T(8,128)(2,1)} %get-tuple-element.28, bf16[1024,8,3,64]{0,3,2,1:T(8,128)(2,1)S(1)} %copy-done), kind=kOutput, calls=%fused_computation.69 | convolution fusion | flops 25794969600 | bytes 128983040 | tf_op jit(solution)/shard_map/bshjc,dhjc->bsd/dot_general | solution.py:94
  2007.1 1454.8 %all-reduce.10.cloned.1.call-done = (f32[32,256,1024]{2,1,0:T(8,128)}, f32[32,256,1024]{2,1,0:T(8,128)}) async-done(((f32[32,256,1024]{2,1,0:T(8,128)}, f32[32,256,1024]{2,1,0:T(8,128)}), (f32[32,256,1024]{2,1,0:T(8,128)}, f32[32,256,1024]{2,1,0:T(8,128)})) %all-reduce.10.cloned.1.call-update) | async-done | bytes 67108880 | tf_op jit(solution)/shard_map/psum | solution.py:72
  3461.9 43.1 fusion.52
  3505.0 1.1 copy.77
  3506.2 15.8 fusion.104
  3522.1 19.0 fusion.154
  3541.1 33.5 fusion.98
  3574.6 52.8 %convolution_bitcast_fusion = f32[2048,1024]{1,0:T(8,128)} fusion(bf16[32,256,1024]{2,1,0:T(8,128)(2,1)} %param.29, f32[32,256,2048]{2,1,0:T(8,128)} %get-tuple-element.62, bf16[32,256,2048]{2,1,0:T(8,128)(2,1)} %get-tuple-element.63), kind=kOutput, calls=%fused_computation.120 | convolution fusion | flops 34426847232 | bytes 125829120 | tf_op jit(solution)/shard_map/bsf,bsd->fd/dot_general | solution.py:80
  3627.6 46.1 %convolution_bitcast_fusion.1 = f32[1024,2048]{1,0:T(8,128)} fusion(bf16[32,256,2048]{2,1,0:T(8,128)(2,1)} %get-tuple-element.67, f32[1024]{0:T(1024)S(1)} %copy-done.32, f32[1024]{0:T(1024)S(1)} %copy-done.30, f32[32,256]{1,0:T(8,128)S(1)} %copy-done.10, f32[32,256,1024]{2,1,0:T(8,128)} %all-reduce.8.cloned.1.call-done, f32[32,256]{1,0:T(8,128)S(1)} %copy-done.7), kind=kOutput, calls=%fused_computation.121 | convolution fusion | flops 34401681408 | bytes 75571200 | tf_op jit(solution)/shard_map/bsd,bsf->df/dot_general | solution.py:81
  3674.0 5.9 sort
  3680.0 54.8 %convert_add_fusion = (f32[32,256,1024]{2,1,0:T(8,128)}, bf16[32,256,1024]{2,1,0:T(8,128)(2,1)}, f32[1024]{0:T(1024)S(1)}) fusion(bf16[32,256,1024]{2,1,0:T(8,128)(2,1)} %param.29, f32[32,256,1024]{2,1,0:T(8,128)} %get-tuple-element.26, f32[32,256]{1,0:T(8,128)S(1)} %broadcast_multiply_fusion, f32[32,256]{1,0:T(8,128)S(1)} %broadcast_multiply_fusion.1, ...), kind=kLoop, calls=%fused_computation.64 | loop fusion | flops 100662272 | bytes 167911424 | tf_op jit(solution)/shard_map/add | solution.py:98
  3734.9 179.9 %scatter_custom_fusion = f32[25152,1024]{1,0:T(8,128)} fusion(s32[8192]{0:T(1024)S(1)} %get-tuple-element.14, f32[]{:T(128)} %constant.52.clone.1, f32[8192,1024]{1,0:T(8,128)} %bitcast.152, s32[8192]{0:T(1024)S(1)} %broadcast_clamp_fusion), kind=kCustom, calls=%fused_computation.57 | custom fusion | flops 8388608 | bytes 103023104 | tf_op jit(solution)/shard_map/scatter-add | solution.py:100
  3918.0 24.0 all-reduce.3
  3944.3 5.4 psum.31
  3950.2 498.9 %reduce-scatter.9.cloned.1.call-done = f32[25152,128]{1,0:T(8,128)} async-done(((f32[25152,1024]{1,0:T(8,128)}), f32[25152,128]{1,0:T(8,128)}) %reduce-scatter.9.cloned.1.call-update) | async-done | bytes 12877840 | tf_op jit(solution)/shard_map/reduce_scatter | solution.py:102
  (138 shorter events, 9.0 us)
Async XLA Ops:
  7.2 1178.0 %copy-start = (bf16[1024,8,3,64]{0,3,2,1:T(8,128)(2,1)S(1)}, bf16[1024,8,3,64]{0,3,2,1:T(8,128)(2,1)}, u32[]{:S(2)}) copy-start(bf16[1024,8,3,64]{0,3,2,1:T(8,128)(2,1)} %param.21) | copy-start | bytes 9437188
  7.2 1153.0 %all-reduce.8.cloned.1.call-start = ((), (), s32[]{:S(2)}) async-start(), calls=%async_computation.6 | async-start | bytes 67108864 | tf_op jit(solution)/shard_map/psum | solution.py:49
  167.1 18.8 copy-start.33
  167.1 18.8 copy-start.34
  167.1 19.4 copy-start.35
  167.1 19.4 copy-start.36
  167.1 20.0 copy-start.27
  167.1 20.6 copy-start.26
  185.8 3276.1 %all-reduce.10.cloned.1.call-start = ((), (), s32[]{:S(2)}) async-start(), calls=%async_computation.13 | async-start | bytes 134217728 | tf_op jit(solution)/shard_map/psum | solution.py:72
  185.9 999.3 %copy-start.20 = (f32[1024]{0:T(1024)}, f32[1024]{0:T(1024)S(1)}, u32[]{:S(2)}) copy-start(f32[1024]{0:T(1024)S(1)} %convert_element_type.119) | copy-start | bytes 12292
  186.5 998.7 %copy-start.22 = (f32[1024]{0:T(1024)}, f32[1024]{0:T(1024)S(1)}, u32[]{:S(2)}) copy-start(f32[1024]{0:T(1024)S(1)} %convert_element_type.120) | copy-start | bytes 12292
  187.8 1090.4 %copy-start.11 = (f32[256,16]{0,1:T(8,128)}, f32[256,16]{0,1:T(8,128)S(1)}, u32[]{:S(2)}) copy-start(f32[256,16]{0,1:T(8,128)S(1)} %get-tuple-element.54) | copy-start | bytes 49156
  187.8 1090.4 %copy-start.13 = (f32[256,16]{0,1:T(8,128)}, f32[256,16]{0,1:T(8,128)S(1)}, u32[]{:S(2)}) copy-start(f32[256,16]{0,1:T(8,128)S(1)} %get-tuple-element.55) | copy-start | bytes 49156
  1172.1 47.4 %copy-start.5 = (f32[32,256]{1,0:T(8,128)}, f32[32,256]{1,0:T(8,128)S(1)}, u32[]{:S(2)}) copy-start(f32[32,256]{1,0:T(8,128)S(1)} %broadcast_multiply_fusion.2) | copy-start | bytes 98308
  1185.2 34.3 copy-start.8
  1261.6 22.3 copy-start.18
  1501.9 40.5 copy-start.14
  1530.1 21.0 copy-start.40
  1551.1 19.0 copy-start.6
  1551.1 19.0 copy-start.9
  1551.1 19.0 copy-start.24
  1551.1 19.0 copy-start.28
  1551.1 19.0 copy-start.31
  1551.1 19.0 copy-start.39
  1872.6 42.1 copy-start.1
  1872.6 42.1 copy-start.2
  1872.6 42.1 copy-start.3
  1872.6 42.1 copy-start.4
  1872.6 42.1 copy-start.12
  1927.7 30.6 copy-start.21
  1927.7 30.6 copy-start.29
  2007.0 1454.9 %copy-start.7 = (f32[32,256]{1,0:T(8,128)S(1)}, f32[32,256]{1,0:T(8,128)}, u32[]{:S(2)}) copy-start(f32[32,256]{1,0:T(8,128)} %copy-done.5) | copy-start | bytes 98308
  2007.0 1454.9 %copy-start.10 = (f32[32,256]{1,0:T(8,128)S(1)}, f32[32,256]{1,0:T(8,128)}, u32[]{:S(2)}) copy-start(f32[32,256]{1,0:T(8,128)} %copy-done.8) | copy-start | bytes 98308
  2007.1 1936.3 %reduce-scatter.19.cloned.1.call-start = ((), (), s32[]{:S(2)}) async-start(), calls=%async_computation.12 | async-start | bytes 589824
  3506.1 15.9 copy-start.23
  3506.1 444.1 %reduce-scatter.13.cloned.1.call-start = ((), (), s32[]{:S(2)}) async-start(), calls=%async_computation.9 | async-start | bytes 2359296 | tf_op jit(solution)/shard_map/reduce_scatter | solution.py:106
  3522.0 428.2 %reduce-scatter.11.cloned.1.call-start = ((), (), s32[]{:S(2)}) async-start(), calls=%async_computation.8 | async-start | bytes 7077888 | tf_op jit(solution)/shard_map/reduce_scatter | solution.py:104
  3574.6 53.0 %copy-start.30 = (f32[1024]{0:T(1024)S(1)}, f32[1024]{0:T(1024)}, u32[]{:S(2)}) copy-start(f32[1024]{0:T(1024)} %convert_element_type.131) | copy-start | bytes 12292
  3574.6 53.0 %copy-start.32 = (f32[1024]{0:T(1024)S(1)}, f32[1024]{0:T(1024)}, u32[]{:S(2)}) copy-start(f32[1024]{0:T(1024)} %convert_element_type.132) | copy-start | bytes 12292
  3574.6 375.6 %reduce-scatter.17.cloned.1.call-start = ((), (), s32[]{:S(2)}) async-start(), calls=%async_computation.11 | async-start | bytes 9437184 | tf_op jit(solution)/shard_map/reduce_scatter | solution.py:110
  3627.5 46.5 %copy-start.17 = (s32[4,2,8,128]{3,2,1,0:T(8,128)S(1)}, s32[4,2,8,128]{3,2,1,0:T(8,128)}, u32[]{:S(2)}) copy-start(s32[4,2,8,128]{3,2,1,0:T(8,128)} %get-tuple-element.44) | copy-start | bytes 98308
  3627.5 52.5 %copy-start.37 = (bf16[1024]{0:T(1024)(128)(2,1)S(1)}, bf16[1024]{0:T(1024)(128)(2,1)}, u32[]{:S(2)}) copy-start(bf16[1024]{0:T(1024)(128)(2,1)} %param.28) | copy-start | bytes 6148
  3627.5 52.5 %copy-start.38 = (bf16[1024]{0:T(1024)(128)(2,1)S(1)}, bf16[1024]{0:T(1024)(128)(2,1)}, u32[]{:S(2)}) copy-start(bf16[1024]{0:T(1024)(128)(2,1)} %param.24) | copy-start | bytes 6148
  3627.5 52.5 %copy-start.16 = (f32[32,256]{1,0:T(8,128)S(1)}, f32[32,256]{1,0:T(8,128)}, u32[]{:S(2)}) copy-start(f32[32,256]{1,0:T(8,128)} %get-tuple-element.17) | copy-start | bytes 98308
  3627.5 52.5 %copy-start.15 = (f32[32,256]{1,0:T(8,128)S(1)}, f32[32,256]{1,0:T(8,128)}, u32[]{:S(2)}) copy-start(f32[32,256]{1,0:T(8,128)} %get-tuple-element.20) | copy-start | bytes 98308
  3627.5 322.7 %reduce-scatter.15.cloned.1.call-start = ((), (), s32[]{:S(2)}) async-start(), calls=%async_computation.10 | async-start | bytes 9437184 | tf_op jit(solution)/shard_map/reduce_scatter | solution.py:108
  3673.7 775.4 %reduce-scatter.9.cloned.1.call-start = ((), (), s32[]{:S(2)}) async-start(), calls=%async_computation.7 | async-start | bytes 115900416 | tf_op jit(solution)/shard_map/reduce_scatter | solution.py:102
  3942.1 507.5 %copy-start.42 = (f32[128]{0:T(128)}, f32[128]{0:T(128)S(1)}, u32[]{:S(2)}) copy-start(f32[128]{0:T(128)S(1)} %dynamic-slice.3) | copy-start | bytes 1540
  (3 other events, 7.1 us)
Sparse Core Ops, SparseCore 0:
  185.9 974.2 all-reduce.7
  2007.2 1454.6 all-reduce.9
  3506.2 30.7 reduce-scatter.18
  3540.7 35.3 reduce-scatter.12
  3579.8 55.4 reduce-scatter.10
  3639.2 64.9 reduce-scatter.16
  3708.2 64.9 reduce-scatter.14
  3914.9 534.2 reduce-scatter.8
where the time goes:
time: 4470 us; the launch traced here: 4460 us
  waiting for transfers between devices  2910 us (65%)
  matrix products  876 us (20%)
  other arithmetic  435 us (10%)
  local copies, waits for them, and re-layouts  188 us (4%)
    psum x1, waiting for transfers between devices, device_step(): layer_sum = lax.psum(partial_out, 'tp')  1450 us
    psum x1, waiting for transfers between devices, device_step(): x_float = lax.psum(partial_x.astype(jnp.float32), 'tp')  957 us
    reduce_scatter x1, waiting for transfers between devices, device_step(): lax.psum_scatter(embed_part, 'dp', scatter_dimension=1, tiled=True)  499 us
    scatter-add x3, other arithmetic, device_step(): jax.ops.segment_sum(grad_x.reshape(-1, d_model), seg_ids, num_segments=vo...  186 us
    dot_general x1, matrix products, device_step(): jnp.einsum('bsd,df->bsf', hid_mlp, w_fc1, preferred_element_type=jnp.floa...  178 us
    gather x1, local copies, waits for them, and re-layouts, device_step(): picked = jnp.take(embed_table, jnp.where(in_range, local_ids, 0), axis=0)  157 us
  transfers between devices with their start and end apart: 8, of which 3 were waited for; matrix products, arithmetic and copies ran while one was open for 10% of the time, Pallas kernels for 0%

commit v1 on v0

v1 whole, which is shorter than its diff:
```python
import functools
import jax
import jax.numpy as jnp
from jax import lax
from jax.experimental import pallas as pl
from jax.experimental.pallas import tpu as pltpu
from jax.sharding import PartitionSpec as P

EPS_NORM = 1e-5
ROPE_BASE = 10000.0
CHUNKS = (4, 6, 6)
HALF_ROOT = 0.5 ** 0.5
PDF_SCALE = (2.0 * 3.141592653589793) ** -0.5
F32, BF16 = jnp.float32, jnp.bfloat16


def dot_f32(a, b, dims):
    return lax.dot_general(a, b, (dims, ((), ())), preferred_element_type=F32)


def rope_consts(seq_len, head_dim):
    rot_dim = head_dim // 4
    half_rot = rot_dim // 2
    inv_freq = ROPE_BASE ** (-(jnp.arange(half_rot, dtype=F32) * 2.0) / rot_dim)
    angles = jnp.arange(seq_len, dtype=F32)[:, None] * inv_freq[None, :]
    angles = jnp.concatenate([angles, angles], axis=-1)
    rest = (seq_len, head_dim - rot_dim)
    cos_head = jnp.concatenate([jnp.cos(angles), jnp.ones(rest, F32)], axis=-1)
    sin_head = jnp.concatenate([jnp.sin(angles), jnp.zeros(rest, F32)], axis=-1)
    row = jnp.arange(2 * head_dim)[:, None]
    col = jnp.arange(2 * head_dim)[None, :]
    ch = col % head_dim
    turn = jnp.where((ch < half_rot) & (row == col + half_rot), -1.0, 0.0) + jnp.where((ch >= half_rot) & (ch < rot_dim) & (row == col - half_rot), 1.0, 0.0)
    return jnp.tile(cos_head, (1, 2)), jnp.tile(sin_head, (1, 2)), turn.astype(BF16)


def attention_kernel(head_dim, q_ref, k_ref, v_ref, g_ref, cos_ref, sin_ref, turn_ref, ctx_ref, dq_ref, dk_ref, dv_ref):
    seq_len, width = q_ref.shape[1], q_ref.shape[2]
    pair = 2 * head_dim
    scale = head_dim ** -0.5
    cos, sin, turn = cos_ref[...], sin_ref[...], turn_ref[...]
    low = lax.broadcasted_iota(jnp.int32, (seq_len, pair), 1) < head_dim
    causal = lax.broadcasted_iota(jnp.int32, (seq_len, seq_len), 0) >= lax.broadcasted_iota(jnp.int32, (seq_len, seq_len), 1)

    def rotate(val):
        turned = dot_f32(val, turn, ((1,), (0,)))
        return (val.astype(F32) * cos + turned * sin).astype(BF16)

    def unrotate(grad):
        turned = dot_f32(grad, turn, ((1,), (1,)))
        return (grad.astype(F32) * cos + turned * sin).astype(BF16)

    def step(j, carry):
        cols = pl.ds(pl.multiple_of(j * pair, pair), pair)
        q = rotate(q_ref[0, :, cols])
        k = rotate(k_ref[0, :, cols])
        v = v_ref[0, :, cols]
        g = g_ref[0, :, cols]
        parts = []
        for head in range(2):
            mine = low if head == 0 else jnp.logical_not(low)
            q_h = jnp.where(mine, q, jnp.zeros_like(q))
            g_h = jnp.where(mine, g, jnp.zeros_like(g))
            scores = dot_f32(q_h, k, ((1,), (1,))) * scale
            scores = jnp.where(causal, scores, -1e30)
            top = jnp.max(scores, axis=-1, keepdims=True)
            expo = jnp.exp(scores - top)
            soft = expo * (1.0 / jnp.sum(expo, axis=-1, keepdims=True))
            probs = soft.astype(BF16)
            ctx = dot_f32(probs, v, ((1,), (0,)))
            d_probs = dot_f32(g_h, v, ((1,), (1,))).astype(BF16).astype(F32)
            d_v = dot_f32(probs, g, ((0,), (0,)))
            inner = jnp.sum(soft * d_probs, axis=-1, keepdims=True)
            d_s = (soft * (d_probs - inner) * scale).astype(BF16)
            d_q = dot_f32(d_s, k, ((1,), (0,)))
            d_k = dot_f32(d_s, q, ((0,), (0,)))
            parts.append((ctx, d_q, d_k, d_v))
        ctx, d_q, d_k, d_v = (jnp.where(low, a, b).astype(BF16) for a, b in zip(*parts))
        ctx_ref[0, :, cols] = ctx
        dq_ref[0, :, cols] = unrotate(d_q)
        dk_ref[0, :, cols] = unrotate(d_k)
        dv_ref[0, :, cols] = d_v
        return carry

    lax.fori_loop(0, width // pair, step, 0)


def attention(q, k, v, g, consts, head_dim):
    n, seq_len, width = q.shape
    big = pl.BlockSpec((1, seq_len, width), lambda i: (i, 0, 0))
    const = [pl.BlockSpec(c.shape, lambda i: (0, 0)) for c in consts]
    shape = jax.ShapeDtypeStruct(q.shape, BF16)
    flops = n * (width // head_dim) * 12 * seq_len * seq_len * 2 * head_dim
    return pl.pallas_call(
        functools.partial(attention_kernel, head_dim),
        grid=(n,),
        in_specs=[big] * 4 + const,
        out_specs=[big] * 4,
        out_shape=[shape] * 4,
        compiler_params=pltpu.CompilerParams(dimension_semantics=("arbitrary",), vmem_limit_bytes=40 * 1024 * 1024),
        cost_estimate=pl.CostEstimate(flops=4 * flops, bytes_accessed=16 * q.size, transcendentals=0),
        name="attention",
    )(q, k, v, g, *consts)


def scatter_kernel(has_init, rows, block, counts, *refs):
    n_arr = len(counts)
    ids_refs, g_refs, rest = refs[:n_arr], refs[n_arr:2 * n_arr], refs[2 * n_arr:]
    if has_init:
        init_ref, out_ref, acc0, acc1, sem = rest
    else:
        out_ref, acc0, acc1, sem = rest
    step = pl.program_id(0)
    padded = acc0.shape[0]
    group = 32

    @pl.when(step == 0)
    def _():
        def clear(i, carry):
            at = pl.ds(pl.multiple_of(i * 8, 8), 8)
            acc1[at, :] = jnp.zeros((8, acc1.shape[1]), F32)
            if not has_init:
                acc0[at, :] = jnp.zeros((8, acc0.shape[1]), F32)
            return carry
        lax.fori_loop(0, padded // 8, clear, 0, unroll=8)
        if has_init:
            copy = pltpu.make_async_copy(init_ref, acc0.at[pl.ds(0, rows)], sem)
            copy.start()
            copy.wait()

    first = 0
    for ids_ref, g_ref, count in zip(ids_refs, g_refs, counts):
        def add_block(ids_ref=ids_ref, g_ref=g_ref):
            def add_group(i, carry):
                for u in range(0, group, 2):
                    at = i * group + u
                    r0 = ids_ref[0, 0, at]
                    r1 = ids_ref[0, 0, at + 1]
                    acc0[pl.ds(r0, 1), :] += g_ref[pl.ds(at, 1), :]
                    acc1[pl.ds(r1, 1), :] += g_ref[pl.ds(at + 1, 1), :]
                return carry
            lax.fori_loop(0, block // group, add_group, 0)
        pl.when((step >= first) & (step < first + count))(add_block)
        first += count

    @pl.when(step == pl.num_programs(0) - 1)
    def _():
        def merge(i, carry):
            at = pl.ds(pl.multiple_of(i * 8, 8), 8)
            acc0[at, :] += acc1[at, :]
            return carry
        lax.fori_loop(0, padded // 8, merge, 0, unroll=8)
        copy = pltpu.make_async_copy(acc0.at[pl.ds(0, rows)], out_ref, sem)
        copy.start()
        copy.wait()


def scatter_rows(ids, grads, rows, init=None, block=2048):
    width = grads[0].shape[1]
    counts = [g.shape[0] // block for g in grads]
    total = sum(counts)
    starts = [sum(counts[:i]) for i in range(len(counts))]
    at = [lambda i, f=f, c=c: jnp.clip(i - f, 0, c - 1) for f, c in zip(starts, counts)]
    in_specs = [pl.BlockSpec((1, 1, block), lambda i, m=m: (m(i), 0, 0), memory_space=pltpu.SMEM) for m in at]
    in_specs += [pl.BlockSpec((block, width), lambda i, m=m: (m(i), 0)) for m in at]
    args = [v.reshape(-1, 1, block) for v in ids] + list(grads)
    has_init = init is not None
    if has_init:
        in_specs.append(pl.BlockSpec(memory_space=pl.ANY))
        args.append(init)
    return pl.pallas_call(
        functools.partial(scatter_kernel, has_init, rows, block, counts),
        grid=(total,),
        in_specs=in_specs,
        out_specs=pl.BlockSpec(memory_space=pl.ANY),
        out_shape=jax.ShapeDtypeStruct((rows, width), F32),
        scratch_shapes=[pltpu.VMEM((rows + 8, width), F32), pltpu.VMEM((rows + 8, width), F32), pltpu.SemaphoreType.DMA],
        compiler_params=pltpu.CompilerParams(dimension_semantics=("arbitrary",), vmem_limit_bytes=40 * 1024 * 1024),
        cost_estimate=pl.CostEstimate(flops=total * block * 3000000, bytes_accessed=8 * total * block * width, transcendentals=0),
        name="scatter_rows",
    )(*args)


def solution(mesh):
    arg_specs = (P('dp', None), P('tp', None), P(None), P(None), P(None), P(None), P(None, 'tp', None, None), P('tp', None, None), P('tp', None, None), P(None), P(None, 'tp'), P('tp'), P('tp', None), P(None), P('dp', None, None))
    out_specs = (P('dp', None, None), P('tp', 'dp'), P('dp'), P('dp'), P('dp'), P('dp'), P('dp', 'tp', None, None), P(('tp', 'dp')), P('tp', None, 'dp'), P('dp'), P('dp', 'tp'), P(('tp', 'dp')), P('tp', 'dp'), P('dp'))
    n_dp = mesh.shape['dp']

    def swap(val):
        return lax.ppermute(val, 'tp', [(0, 1), (1, 0)])

    def device_step(token_ids, embed_table, ln1_gain, ln1_bias, ln2_gain, ln2_bias, w_qkv, b_qkv, w_dense, b_dense, w_fc1, b_fc1, w_fc2, b_fc2, cotangent):
        n_seq, seq_len = token_ids.shape
        half_seq = n_seq // 2
        vocab_local, d_model = embed_table.shape
        heads_local, head_dim = w_qkv.shape[1], w_qkv.shape[3]
        attn_local = heads_local * head_dim
        ff_local = w_fc1.shape[1]
        tp_i, dp_i = lax.axis_index('tp'), lax.axis_index('dp')
        own_at, peer_at = tp_i * half_seq, (1 - tp_i) * half_seq
        zero = jnp.where(token_ids[0, 0] < 0, 1.0, 0.0).astype(F32)

        def from_peer(w):
            size = w.shape[0] // n_dp
            piece = swap(lax.dynamic_slice_in_dim(w, dp_i * size, size, 0).astype(F32))
            whole = lax.all_gather(piece, 'dp', axis=0, tiled=True)
            return (whole + zero).astype(BF16)

        def rows_of(ids):
            local = ids - tp_i * vocab_local
            ok = (local >= 0) & (local < vocab_local)
            picked = jnp.take(embed_table, jnp.where(ok, local, 0), axis=0)
            return jnp.where(ok[..., None], picked, jnp.zeros_like(picked)).astype(F32)

        ids_own = lax.dynamic_slice_in_dim(token_ids, own_at, half_seq, 0)
        ids_peer = lax.dynamic_slice_in_dim(token_ids, peer_at, half_seq, 0)
        bounds = []
        start = 0
        for size in CHUNKS:
            bounds.append((start, start + size))
            start += size
        sent_x = [swap(rows_of(ids_peer[a:b].reshape(-1))) for a, b in bounds]

        wqkv_own = w_qkv.transpose(2, 0, 1, 3).reshape(3 * d_model, attn_local)
        wqkv_peer = from_peer(wqkv_own)
        w_q, w_k, w_v = (jnp.concatenate([wqkv_own[i * d_model:(i + 1) * d_model], wqkv_peer[i * d_model:(i + 1) * d_model]], axis=1) for i in range(3))
        fc2_all = jnp.concatenate([w_fc2, from_peer(w_fc2)], axis=0)
        dense_own = w_dense.reshape(attn_local, d_model)
        dense_all = jnp.concatenate([dense_own, from_peer(dense_own)], axis=0)
        fc1_all = jnp.concatenate([w_fc1, from_peer(w_fc1)], axis=1)
        bqkv_own = b_qkv.transpose(1, 0, 2).reshape(-1)
        bias_own = jnp.concatenate([bqkv_own, b_fc1]).astype(F32)
        bias_peer = swap(bias_own)
        b_q, b_k, b_v = (jnp.concatenate([bias_own[i * attn_local:(i + 1) * attn_local], bias_peer[i * attn_local:(i + 1) * attn_local]]) for i in range(3))
        bfc1_all = jnp.concatenate([bias_own[3 * attn_local:], bias_peer[3 * attn_local:]])

        gain1, gain2 = ln1_gain.astype(F32), ln2_gain.astype(F32)
        shift1, shift2 = ln1_bias.astype(F32), ln2_bias.astype(F32)
        out_bias = b_dense.astype(F32) + b_fc2.astype(F32)
        consts = rope_consts(seq_len, head_dim)
        ids_all = lax.all_gather(token_ids, 'dp', axis=0)
        local_all = ids_all - tp_i * vocab_local
        local_all = jnp.where((local_all >= 0) & (local_all < vocab_local), local_all, vocab_local)
        local_own = lax.dynamic_slice_in_dim(local_all, own_at, half_seq, 1)
        local_peer = lax.dynamic_slice_in_dim(local_all, peer_at, half_seq, 1)
        cot_own = lax.dynamic_slice_in_dim(cotangent, own_at, half_seq, 0)

        layer_out = jnp.zeros(cotangent.shape, BF16)
        scatter_parts = []
        dw_sum = None
        after, held, older = None, [], []
        small_sum = None
        for (a, b), recv_x in zip(bounds, sent_x):
            tokens = (b - a) * seq_len
            flat = lambda v: v.reshape(tokens, v.shape[-1])
            cot = flat(cot_own[a:b])
            if after is not None:
                cot, recv_x, _ = lax.optimization_barrier((cot, recv_x, after + older))
                older = late
            grad_act = dot_f32(cot, fc2_all, ((1,), (1,))).astype(BF16)
            grad_ctx = dot_f32(cot, dense_all, ((1,), (1,))).astype(BF16)
            x = rows_of(ids_own[a:b].reshape(-1)) + recv_x
            centered = x - jnp.mean(x, axis=-1, keepdims=True)
            inv_std = lax.rsqrt(jnp.mean(centered * centered, axis=-1, keepdims=True) + EPS_NORM)
            normed = centered * inv_std
            hid1 = (normed * gain1 + shift1).astype(BF16)
            hid2 = (normed * gain2 + shift2).astype(BF16)
            q, k, v = ((dot_f32(hid1, w, ((1,), (0,))) + bias).astype(BF16).reshape(b - a, seq_len, -1) for w, bias in ((w_q, b_q), (w_k, b_k), (w_v, b_v)))
            ctx, d_q, d_k, d_v = (flat(r) for r in attention(q, k, v, grad_ctx.reshape(b - a, seq_len, -1), consts, head_dim))
            pre_low = (dot_f32(hid2, fc1_all, ((1,), (0,))) + bfc1_all).astype(BF16)
            grad_act, pre_low = lax.optimization_barrier((grad_act, pre_low))
            pre_act = pre_low.astype(F32)
            cdf = 0.5 + 0.5 * lax.erf(pre_act * HALF_ROOT)
            act = (pre_act * cdf).astype(BF16)
            slope = cdf + pre_act * (jnp.exp(-0.5 * pre_act * pre_act) * PDF_SCALE)
            grad_pre = (grad_act.astype(F32) * slope).astype(BF16)
            out_sum = x + dot_f32(ctx, dense_all, ((1,), (0,))) + dot_f32(act, fc2_all, ((1,), (0,)))
            recv_out = swap(out_sum)
            as_out = lambda v: (v + out_bias).astype(BF16).reshape(b - a, seq_len, d_model)
            layer_out = lax.dynamic_update_slice_in_dim(layer_out, as_out(out_sum), own_at + a, 0)
            layer_out = lax.dynamic_update_slice_in_dim(layer_out, as_out(recv_out), peer_at + a, 0)

            if held:
                out_sum, act, grad_pre, d_q, d_k, d_v, _ = lax.optimization_barrier((out_sum, act, grad_pre, d_q, d_k, d_v, held))
                held = []
            grad_h2 = dot_f32(grad_pre, fc1_all, ((1,), (1,))).astype(BF16).astype(F32)
            grad_h1 = (dot_f32(d_q, w_q, ((1,), (1,))) + dot_f32(d_k, w_k, ((1,), (1,))) + dot_f32(d_v, w_v, ((1,), (1,)))).astype(BF16).astype(F32)
            grad_norm = grad_h1 * gain1 + grad_h2 * gain2
            grad_x = cot.astype(F32) + inv_std * (grad_norm - jnp.mean(grad_norm, axis=-1, keepdims=True) - normed * jnp.mean(grad_norm * normed, axis=-1, keepdims=True))
            by_col = grad_x.reshape(tokens, n_dp, d_model // n_dp).transpose(1, 0, 2)
            mine = lax.all_to_all(by_col, 'dp', split_axis=0, concat_axis=0, tiled=True)
            theirs = swap(mine)
            after, held, late = [by_col, out_sum], [mine, recv_out], [theirs]
            scatter_parts.append((local_own[:, a:b].reshape(-1), mine.reshape(-1, d_model // n_dp), local_peer[:, a:b].reshape(-1), theirs.reshape(-1, d_model // n_dp)))

            if b == half_seq:
                hid1, hid2, ctx, act, grad_pre, d_q, d_k, d_v, _ = lax.optimization_barrier((hid1, hid2, ctx, act, grad_pre, d_q, d_k, d_v, by_col))
            t0 = ((0,), (0,))
            hid_fc1, pre_fc1 = hid2, grad_pre
            if b == half_seq:
                hid_fc1, pre_fc1, _ = lax.optimization_barrier((hid2, grad_pre, [mine, recv_out]))
            dws = [dot_f32(hid1, d_q, t0), dot_f32(hid1, d_k, t0), dot_f32(hid1, d_v, t0), dot_f32(ctx, cot, t0), dot_f32(hid_fc1, pre_fc1, t0), dot_f32(act, cot, t0)]
            total = lambda v: jnp.sum(v.astype(F32), axis=0)
            smalls = [total(grad_h1 * normed), total(grad_h1), total(grad_h2 * normed), total(grad_h2), total(cot), total(d_q), total(d_k), total(d_v), total(grad_pre)]
            dw_sum = dws if dw_sum is None else [p + r for p, r in zip(dw_sum, dws)]
            small_sum = smalls if small_sum is None else [p + r for p, r in zip(small_sum, smalls)]

        pick = lambda parts, i: [p for part in parts for p in (part[i], part[i + 2])]
        embed_first = scatter_rows(pick(scatter_parts[:-1], 0), pick(scatter_parts[:-1], 1), vocab_local)
        sum_embed = scatter_rows(pick(scatter_parts[-1:], 0), pick(scatter_parts[-1:], 1), vocab_local, embed_first)

        d_wq, d_wk, d_wv, d_dense, d_fc1, d_fc2 = dw_sum
        rs = lambda v, dim: lax.psum_scatter(v, 'dp', scatter_dimension=dim, tiled=True)
        r_fc2, r_fc1, r_dense = rs(d_fc2, 1), rs(d_fc1, 0), rs(d_dense, 1)
        r_q, r_k, r_v = rs(d_wq, 0), rs(d_wk, 0), rs(d_wv, 0)
        sum_fc2 = r_fc2[:ff_local] + swap(r_fc2[ff_local:])
        sum_fc1 = r_fc1[:, :ff_local] + swap(r_fc1[:, ff_local:])
        sum_dense = (r_dense[:attn_local] + swap(r_dense[attn_local:])).reshape(heads_local, head_dim, -1)
        own_qkv = jnp.stack([r[:, :attn_local].reshape(-1, heads_local, head_dim) for r in (r_q, r_k, r_v)], axis=2)
        peer_qkv = jnp.stack([r[:, attn_local:] for r in (r_q, r_k, r_v)])
        got_qkv = swap(peer_qkv).reshape(3, -1, heads_local, head_dim).transpose(1, 2, 0, 3)
        sum_qkv = own_qkv + got_qkv

        s_bqkv = [v.reshape(2, heads_local, head_dim) for v in small_sum[5:8]]
        bqkv_grad = jnp.stack(s_bqkv, axis=2)
        fc1_bias = small_sum[8].reshape(2, -1)
        pieces = small_sum[:5] + [bqkv_grad[0].reshape(-1), fc1_bias[0], bqkv_grad[1].reshape(-1), fc1_bias[1]]
        packed = jnp.concatenate([p.reshape(n_dp, -1) for p in pieces], axis=1)
        got = rs(packed, 0)[0]
        n_common = 5 * d_model // n_dp
        n_side = (3 * attn_local + ff_local) // n_dp
        common, side_own, side_peer = got[:n_common], got[n_common:n_common + n_side], got[n_common + n_side:]
        moved = swap(jnp.concatenate([common, side_peer]))
        common = (common + moved[:n_common]).reshape(5, -1)
        side = side_own + moved[n_common:]
        sum_bqkv, sum_bfc1 = side[:3 * attn_local // n_dp], side[3 * attn_local // n_dp:]
        return (layer_out, sum_embed, common[0], common[1], common[2], common[3], sum_qkv, sum_bqkv, sum_dense, common[4], sum_fc1, sum_bfc1, sum_fc2, common[4])

    return jax.shard_map(device_step, mesh=mesh, in_specs=arg_specs, out_specs=out_specs, check_vma=False)
```

time: 4470 us -> 2080 us (0.47)
  waiting for transfers between devices: 2910 us -> 453 us
  Pallas kernels: 0 us -> 376 us
  matrix products: 876 us -> 547 us
  starting transfers between devices: 0.5 us -> 272 us
  other arithmetic: 435 us -> 175 us
    psum x2 -> x0, waiting for transfers between devices: 2410 us -> none  [the longest x1 1450 us: device_step(): layer_sum = lax.psum(partial_out, 'tp')]
    reduce_scatter x5 -> x6, waiting for transfers between devices: 499 us -> 0.05 us  [device_step(): lax.psum_scatter(v, 'dp', scatter_dimension=dim, tiled=True)]
    ppermute x0 -> x19, waiting for transfers between devices: none -> 453 us  [swap(): return lax.ppermute(val, 'tp', [(0, 1), (1, 0)])]
    pallas_call x0 -> x5, Pallas kernels: none -> 376 us  [the longest x3 201 us: attention(): pl.pallas_call(functools.partial(attention_kernel, head_dim), grid=(n,),...]
    dot_general x17 -> x54, matrix products: 844 us -> 547 us  [dot_f32(): return lax.dot_general(a, b, (dims, ((), ())), preferred_element_type=F32)]
    ppermute x0 -> x19, starting transfers between devices: none -> 256 us  [swap(): return lax.ppermute(val, 'tp', [(0, 1), (1, 0)])]
    scatter-add x3 -> x0, other arithmetic: 186 us -> none  [device_step(): jax.ops.segment_sum(grad_x.reshape(-1, d_model), seg_ids, num_segments=vo...]
    gather x1 -> x6, local copies, waits for them, and re-layouts: 157 us -> 82.5 us  [rows_of(): picked = jnp.take(embed_table, jnp.where(ok, local, 0), axis=0)]
  transfers between devices with their start and end apart: 8 -> 32, of which waited for: 3 -> 8; matrix products, arithmetic and copies ran while one was open for 10% -> 39% of each run, Pallas kernels for 0% -> 18%
where the time goes in v1:
time: 2080 us; the launch traced here: 2040 us
  matrix products  547 us (26%)
  waiting for transfers between devices  453 us (22%)
  Pallas kernels  376 us (18%)
  starting transfers between devices  272 us (13%)
  other arithmetic  175 us (8%)
  local copies, waits for them, and re-layouts  166 us (8%)
  blocking collectives  35.2 us (2%)
    dot_general x54, matrix products, dot_f32(): return lax.dot_general(a, b, (dims, ((), ())), preferred_element_type=F32)  547 us
    ppermute x19, waiting for transfers between devices, swap(): return lax.ppermute(val, 'tp', [(0, 1), (1, 0)])  453 us
    ppermute x19, starting transfers between devices, swap(): return lax.ppermute(val, 'tp', [(0, 1), (1, 0)])  256 us
    pallas_call x3, Pallas kernels, attention(): pl.pallas_call(functools.partial(attention_kernel, head_dim), grid=(n,),...  201 us
    pallas_call x2, Pallas kernels, scatter_rows(): pl.pallas_call(functools.partial(scatter_kernel, has_init, rows, block, c...  175 us
    gather x6, local copies, waits for them, and re-layouts, rows_of(): picked = jnp.take(embed_table, jnp.where(ok, local, 0), axis=0)  82.5 us
    reduce_sum x15, other arithmetic, device_step(): total = lambda v: jnp.sum(v.astype(F32), axis=0)  59 us
  transfers between devices with their start and end apart: 32, of which 8 were waited for; matrix products, arithmetic and copies ran while one was open for 39% of the time, Pallas kernels for 18%

profile of v1, /device:TPU:0, one launch (start us, length us, event | category | flops | bytes accessed | tf_op | source)
XLA Modules:
  0.0 2042.7 jit_solution(11738745173629464726)
XLA Ops:
  26.8 17.0 collective-permute-done.1
  47.4 22.1 %collective-permute-done.4 = f32[256,1024]{1,0:T(8,128)S(1)} collective-permute-done((f32[256,1024]{1,0:T(8,128)S(1)}, f32[256,1024]{1,0:T(8,128)S(1)}, u32[]{:S(2)}, u32[]{:S(2)}) %collective-permute-start.4) | collective-permute-done | bytes 1048608 | tf_op jit(solution)/shard_map/ppermute | solution.py:190
  70.9 14.9 gather_fusion.1
  88.4 30.9 %collective-permute-start = (f32[1024,1024]{1,0:T(8,128)}, f32[1024,1024]{1,0:T(8,128)}, u32[]{:S(2)}, u32[]{:S(2)}) collective-permute-start(f32[1024,1024]{1,0:T(8,128)} %fusion.44), channel_id=1, source_target_pairs={{0,8},{8,0},{1,9},{9,1},{2,10},{10,2},{3,11},{11,3},{4,12},{12,4},... | collective-permute-start | bytes 12582920 | tf_op jit(solution)/shard_map/ppermute | solution.py:190
  123.7 11.4 gather_fusion.3
  138.7 43.9 %collective-permute-start.7 = (f32[1536,1024]{1,0:T(8,128)}, f32[1536,1024]{1,0:T(8,128)}, u32[]{:S(2)}, u32[]{:S(2)}) collective-permute-start(f32[1536,1024]{1,0:T(8,128)} %fusion.42), channel_id=1, source_target_pairs={{0,8},{8,0},{1,9},{9,1},{2,10},{10,2},{3,11},{11,3},{4,12},{12,4},... | collective-permute-start | bytes 18874376 | tf_op jit(solution)/shard_map/ppermute | solution.py:190
  182.7 11.4 gather_fusion.5
  197.8 43.7 %collective-permute-start.9 = (f32[1536,1024]{1,0:T(8,128)}, f32[1536,1024]{1,0:T(8,128)}, u32[]{:S(2)}, u32[]{:S(2)}) collective-permute-start(f32[1536,1024]{1,0:T(8,128)} %fusion.41), channel_id=1, source_target_pairs={{0,8},{8,0},{1,9},{9,1},{2,10},{10,2},{3,11},{11,3},{4,12},{12,4},... | collective-permute-start | bytes 18874376 | tf_op jit(solution)/shard_map/ppermute | solution.py:190
  256.8 20.2 gather_fusion
  277.4 12.5 gather_fusion.2
  289.8 12.2 gather_fusion.4
  332.7 50.5 %attention.3 = (bf16[4,256,1024]{2,1,0:T(8,128)(2,1)S(1)}, bf16[4,256,1024]{2,1,0:T(8,128)(2,1)S(1)}, bf16[4,256,1024]{2,1,0:T(8,128)(2,1)S(1)}, bf16[4,256,1024]{2,1,0:T(8,128)(2,1)S(1)}) custom-call(bf16[4,256,1024]{2,1,0:T(8,128)(2,1)S(1)} %bitcast.211, bf16[4,256,1024]{2,1,0:T(8,128)(2,1)S(1)} %bitcast.210, bf16[4,256,1024]{2,1,0:T(8,128)(2,1)} %bitcast.290, ...), custom_call_target="tpu_custom_call" | custom-call | flops 25769803776 | bytes 16777216 | tf_op jit(solution)/shard_map/attention/pallas_call | solution.py:94
  407.1 13.5 convolution_convert_fusion.2
  427.3 11.6 add_convert_fusion.2
  438.9 14.3 convert_reduce_fusion.2
  453.2 17.4 fusion.37
  475.8 21.2 %add_add_fusion.7 = f32[1024,1024]{1,0:T(8,128)} fusion(f32[1024,1024]{1,0:T(8,128)} %copy-done.37, f32[1024,1024]{1,0:T(8,128)} %fusion.66, f32[1024,4096]{1,0:T(8,128)} %get-tuple-element.148, bf16[1024,4096]{1,0:T(8,128)(2,1)} %add_convert_fusion.2, bf16[2048,1024]{1,0:T(8,128)(2,1)} %copy-done.54, bf16[2048,1024]{1,0:T(8,128)(2,1)} %param.31), kind=kOutput, calls=%fused_computation.147 | convolution fusion | flops 8621391872 | bytes 46137344 | tf_op jit(solution)/shard_map/dot_general | solution.py:18
  504.4 21.1 %add_convert_fusion.1 = bf16[1536,4096]{1,0:T(8,128)(2,1)} fusion(f32[4096]{0:T(1024)S(1)} %pad_maximum_fusion.9, f32[1024]{0:T(1024)S(1)} %convert_element_type.305, f32[1024]{0:T(1024)S(1)} %convert_element_type.304, bf16[1024,2048]{1,0:T(8,128)(2,1)} %copy-done.53, bf16[1024,2048]{1,0:T(8,128)(2,1)} %param.29, f32[1536,1024]{1,0:T(8,128)} %copy-done.36, ...), kind=kOutput, calls=%fused_computation.42 | convolution fusion | flops 12922126336 | bytes 27299840 | tf_op jit(solution)/shard_map/dot_general | solution.py:18
  547.2 19.1 convolution_convert_fusion.1
  577.6 116.1 %collective-permute-start.6 = (f32[1024,1024]{1,0:T(8,128)}, f32[1024,1024]{1,0:T(8,128)}, u32[]{:S(2)}, u32[]{:S(2)}) collective-permute-start(f32[1024,1024]{1,0:T(8,128)} %add_add_fusion.7), channel_id=1, source_target_pairs={{0,8},{8,0},{1,9},{9,1},{2,10},{10,2},{3,11},{11,3},{4,12},{12,4},... | collective-permute-start | bytes 12582920 | tf_op jit(solution)/shard_map/ppermute | solution.py:190
  693.6 24.1 %fusion.8 = (bf16[1536,4096]{1,0:T(8,128)(2,1)}, bf16[1536,4096]{1,0:T(8,128)(2,1)}) fusion(bf16[1536,4096]{1,0:T(8,128)(2,1)} %add_convert_fusion.1, bf16[1536,4096]{1,0:T(8,128)(2,1)} %convolution_convert_fusion.1), kind=kLoop, calls=%fused_computation.29 | loop fusion | flops 88080384 | bytes 50331648 | tf_op jit(solution)/shard_map/convert_element_type | solution.py:276
  717.8 75.4 %attention.4 = (bf16[6,256,1024]{2,1,0:T(8,128)(2,1)S(1)}, bf16[6,256,1024]{2,1,0:T(8,128)(2,1)S(1)}, bf16[6,256,1024]{2,1,0:T(8,128)(2,1)S(1)}, bf16[6,256,1024]{2,1,0:T(8,128)(2,1)S(1)}) custom-call(bf16[6,256,1024]{2,1,0:T(8,128)(2,1)} %bitcast.283, bf16[6,256,1024]{2,1,0:T(8,128)(2,1)} %bitcast.282, bf16[6,256,1024]{2,1,0:T(8,128)(2,1)} %bitcast.281, ...), custom_call_target="tpu_custom_call" | custom-call | flops 38654705664 | bytes 25165824 | tf_op jit(solution)/shard_map/attention/pallas_call | solution.py:94
  798.8 20.1 add_add_fusion.3
  842.9 25.7 %fusion.31 = (f32[1024]{0:T(1024)}, f32[1536]{0:T(1024)S(1)}, f32[1024]{0:T(1024)}, f32[1536]{0:T(1024)S(1)}, f32[1024]{0:T(1024)}, /*index=5*/f32[1024]{0:T(1024)}, bf16[1536,1024]{1,0:T(8,128)(2,1)}) fusion(f32[1536]{0:T(1024)S(1)} %copy-done.115, f32[1536,1024]{1,0:T(8,128)} %copy-done.36, f32[1536]{0:T(1024)S(1)} %copy-done.107, ...), kind=kOutput, calls=%fused_computation.83 | convolution fusion | flops 12928411648 | bytes 33603584 | tf_op jit(solution)/shard_map/dot_general | solution.py:18
  884.1 162.3 %collective-permute-done.10 = f32[8,1024,128]{2,1,0:T(8,128)} collective-permute-done((f32[8,1024,128]{2,1,0:T(8,128)}, f32[8,1024,128]{2,1,0:T(8,128)}, u32[]{:S(2)}, u32[]{:S(2)}) %collective-permute-start.10) | collective-permute-done | bytes 4194336 | tf_op jit(solution)/shard_map/ppermute | solution.py:190
  1072.0 20.5 %convolution_convert_fusion = bf16[1536,4096]{1,0:T(8,128)(2,1)} fusion(bf16[1536,1024]{1,0:T(8,128)(2,1)} %bitcast.225, bf16[2048,1024]{1,0:T(8,128)(2,1)} %copy-done.54, bf16[2048,1024]{1,0:T(8,128)(2,1)} %param.31), kind=kOutput, calls=%fused_computation.56 | convolution fusion | flops 12907970560 | bytes 24117248 | tf_op jit(solution)/shard_map/dot_general | solution.py:18
  1092.5 7.6 convolution_convert_fusion.5
  1100.2 19.1 add_convert_fusion
  1119.3 75.5 %attention.5 = (bf16[6,256,1024]{2,1,0:T(8,128)(2,1)S(1)}, bf16[6,256,1024]{2,1,0:T(8,128)(2,1)S(1)}, bf16[6,256,1024]{2,1,0:T(8,128)(2,1)S(1)}, bf16[6,256,1024]{2,1,0:T(8,128)(2,1)S(1)}) custom-call(bf16[6,256,1024]{2,1,0:T(8,128)(2,1)} %bitcast.287, bf16[6,256,1024]{2,1,0:T(8,128)(2,1)} %bitcast.286, bf16[6,256,1024]{2,1,0:T(8,128)(2,1)} %bitcast.285, ...), custom_call_target="tpu_custom_call" | custom-call | flops 38654705664 | bytes 25165824 | tf_op jit(solution)/shard_map/attention/pallas_call | solution.py:94
  1205.9 16.0 fusion.17
  1221.9 20.3 add_add_fusion.2
  1256.9 25.7 %fusion.34 = (f32[1024]{0:T(1024)}, f32[1536]{0:T(1024)S(1)}, f32[1024]{0:T(1024)}, f32[1536]{0:T(1024)S(1)}, f32[1024]{0:T(1024)}, /*index=5*/f32[1024]{0:T(1024)}, bf16[1536,1024]{1,0:T(8,128)(2,1)}) fusion(f32[1536]{0:T(1024)S(1)} %copy-done.113, f32[1536,1024]{1,0:T(8,128)} %copy-done.35, f32[1536]{0:T(1024)S(1)} %copy-done.105, ...), kind=kOutput, calls=%fused_computation.86 | convolution fusion | flops 12928411648 | bytes 33603584 | tf_op jit(solution)/shard_map/dot_general | solution.py:18
  1282.6 7.3 convert_reduce_fusion.7
  1332.8 21.7 %fusion.58 = f32[4096,1024]{1,0:T(8,128)} fusion(bf16[1024,1024]{1,0:T(8,128)(2,1)} %bitcast.235, f32[1024,4096]{1,0:T(8,128)} %get-tuple-element.148, bf16[1024,4096]{1,0:T(8,128)(2,1)} %add_convert_fusion.2), kind=kOutput, calls=%fused_computation.291 | convolution fusion | flops 8602517504 | bytes 44040192 | tf_op jit(solution)/shard_map/dot_general | solution.py:18
  1368.3 21.3 %fusion.104 = f32[4096,1024]{1,0:T(8,128)} fusion(bf16[1536,4096]{1,0:T(8,128)(2,1)} %get-tuple-element.98, bf16[1536,1024]{1,0:T(8,128)(2,1)} %bitcast.231), kind=kOutput, calls=%fused_computation.331 | convolution fusion | flops 12884901888 | bytes 32505856 | tf_op jit(solution)/shard_map/dot_general | solution.py:18
  1389.6 26.5 %add_add_fusion = f32[4096,1024]{1,0:T(8,128)} fusion(f32[4096,1024]{1,0:T(8,128)} %fusion.58, f32[4096,1024]{1,0:T(8,128)} %fusion.104, bf16[1536,4096]{1,0:T(8,128)(2,1)} %get-tuple-element.99, bf16[1536,1024]{1,0:T(8,128)(2,1)S(1)} %bitcast.229), kind=kOutput, calls=%fused_computation.52 | convolution fusion | flops 12893290496 | bytes 66060288 | tf_op jit(solution)/shard_map/dot_general | solution.py:18
  1421.3 17.1 fusion.46
  1438.5 22.1 %fusion.45 = f32[1024,4096]{1,0:T(8,128)} fusion(bf16[1536,4096]{1,0:T(8,128)(2,1)} %get-tuple-element.75, f32[1024]{0:T(1024)S(1)} %copy-done.128, f32[1024]{0:T(1024)S(1)} %copy-done.111, f32[1536,1024]{1,0:T(8,128)} %copy-done.36, f32[1536]{0:T(1024)S(1)} %copy-done.116, f32[1536]{0:T(1024)S(1)} %copy-done.108), kind=kOutput, calls=%fused_computation.180 | convolution fusion | flops 12892766208 | bytes 35672064 | tf_op jit(solution)/shard_map/dot_general | solution.py:18
  1460.6 92.4 %collective-permute-done.11 = f32[1536,1024]{1,0:T(8,128)} collective-permute-done((f32[1536,1024]{1,0:T(8,128)}, f32[1536,1024]{1,0:T(8,128)}, u32[]{:S(2)}, u32[]{:S(2)}) %collective-permute-start.11) | collective-permute-done | bytes 6291488 | tf_op jit(solution)/shard_map/ppermute | solution.py:190
  1553.0 29.0 %add_add_fusion.1 = f32[1024,4096]{1,0:T(8,128)} fusion(f32[1024,4096]{1,0:T(8,128)} %fusion.46, f32[1024,4096]{1,0:T(8,128)} %fusion.45, bf16[1536,1024]{1,0:T(8,128)(2,1)} %copy-done.39, bf16[1536,4096]{1,0:T(8,128)(2,1)} %get-tuple-element.97), kind=kOutput, calls=%fused_computation.53 | convolution fusion | flops 12893290496 | bytes 66060288 | tf_op jit(solution)/shard_map/dot_general | solution.py:18
  1582.7 10.2 all-gather
  1635.1 25.0 %all-reduce.2 = f32[8,1536]{1,0:T(8,128)S(1)} all-reduce(f32[8,1536]{1,0:T(8,128)S(1)} %concatenate.62), channel_id=3, replica_groups=mesh['tp'=2,'dp'=8] {'dp'}, use_global_device_ids=true, to_apply=%region_39.42.clone | all-reduce | flops 12288 | bytes 98304
  1666.1 105.2 %collective-permute-done.14 = f32[1088]{0:T(1024)S(1)} collective-permute-done((f32[1088]{0:T(1024)S(1)}, f32[1088]{0:T(1024)S(1)}, u32[]{:S(2)}, u32[]{:S(2)}) %collective-permute-start.14) | collective-permute-done | bytes 4384 | tf_op jit(solution)/shard_map/ppermute | solution.py:190
  1773.1 10.1 add_convert_fusion.6
  1798.7 101.9 %scatter_rows.2.refs_4_ = f32[25152,128]{1,0:T(8,128)} custom-call(s32[4,1,2048]{2,1,0:T(1,128)S(1)} %reshape_reshape.20.refs_0_, s32[4,1,2048]{2,1,0:T(1,128)S(1)} %reshape_reshape.21.refs_1_, s32[6,1,2048]{2,1,0:T(1,128)S(1)} %reshape_reshape.26.refs_2_, s32[6,1,2048]{2,1,0:T(1,128)S(1)} %reshape_reshape.27.refs_3_, f32[8192,128]{1,0:T(8,128)} %bitcast.48.refs_4_, ...), custom_call_target="tpu_custom_call" | custom-call | flops 122880000000 | bytes 41943040 | tf_op jit(solution)/shard_map/scatter_rows/pallas_call | solution.py:171
  1901.0 34.1 %collective-permute-done.16 = f32[512,128]{1,0:T(8,128)} collective-permute-done((f32[512,128]{1,0:T(8,128)}, f32[512,128]{1,0:T(8,128)}, u32[]{:S(2)}, u32[]{:S(2)}) %collective-permute-start.16) | collective-permute-done | bytes 262176 | tf_op jit(solution)/shard_map/ppermute | solution.py:190
  1936.7 13.8 collective-permute-done.15
  1960.1 72.9 %scatter_rows.3 = f32[25152,128]{1,0:T(8,128)} custom-call(s32[6,1,2048]{2,1,0:T(1,128)S(1)} %reshape_reshape.24.refs_0_, s32[6,1,2048]{2,1,0:T(1,128)S(1)} %reshape_reshape.25.refs_1_, f32[12288,128]{1,0:T(8,128)} %bitcast.46.refs_2_, f32[12288,128]{1,0:T(8,128)} %bitcast.47.refs_3_, f32[25152,128]{1,0:T(8,128)} %scatter_rows.2.refs_4_), custom_call_target="tpu_custom_call" | custom-call | flops 73728000000 | bytes 25165824 | tf_op jit(solution)/shard_map/scatter_rows/pallas_call | solution.py:171
  (627 shorter events, 397.3 us)
Async XLA Ops:
  7.2 295.7 %all-gather.8.cloned.1.call-start = ((), (), s32[]{:S(2)}) async-start(), calls=%async_computation.10 | async-start | bytes 2359296 | tf_op jit(solution)/shard_map/all_gather | solution.py:206
  8.2 9.7 collective-permute-start.3
  18.5 299.1 %all-gather.6.cloned.1.call-start = ((), (), s32[]{:S(2)}) async-start(), calls=%async_computation.9 | async-start | bytes 7077888 | tf_op jit(solution)/shard_map/all_gather | solution.py:206
  25.0 18.7 collective-permute-start.1
  44.7 355.8 %all-gather.10.cloned.1.call-start = ((), (), s32[]{:S(2)}) async-start(), calls=%async_computation.11 | async-start | bytes 9437184 | tf_op jit(solution)/shard_map/all_gather | solution.py:206
  45.9 23.6 %collective-permute-start.4 = (f32[256,1024]{1,0:T(8,128)S(1)}, f32[256,1024]{1,0:T(8,128)S(1)}, u32[]{:S(2)}, u32[]{:S(2)}) collective-permute-start(f32[256,1024]{1,0:T(8,128)S(1)} %dynamic-slice_convert_fusion.1), channel_id=1, source_target_pairs={{0,8},{8,0},{1,9},{9,1},{2,10},{10,2},{3,11},{11,3},{4,12},{12,4},... | collective-permute-start | bytes 3145736 | tf_op jit(solution)/shard_map/ppermute | solution.py:190
  70.6 350.0 %all-gather.12.cloned.1.call-start = ((), (), s32[]{:S(2)}) async-start(), calls=%async_computation.12 | async-start | bytes 9437184 | tf_op jit(solution)/shard_map/all_gather | solution.py:206
  88.4 221.7 %collective-permute-start = (f32[1024,1024]{1,0:T(8,128)}, f32[1024,1024]{1,0:T(8,128)}, u32[]{:S(2)}, u32[]{:S(2)}) collective-permute-start(f32[1024,1024]{1,0:T(8,128)} %fusion.44), channel_id=1, source_target_pairs={{0,8},{8,0},{1,9},{9,1},{2,10},{10,2},{3,11},{11,3},{4,12},{12,4},... | collective-permute-start | bytes 12582920 | tf_op jit(solution)/shard_map/ppermute | solution.py:190
  119.4 183.3 %collective-permute-start.2 = (f32[3584]{0:T(1024)S(1)}, f32[3584]{0:T(1024)S(1)}, u32[]{:S(2)}, u32[]{:S(2)}) collective-permute-start(f32[3584]{0:T(1024)S(1)} %maximum_convert_fusion), channel_id=1, source_target_pairs={{0,8},{8,0},{1,9},{9,1},{2,10},{10,2},{3,11},{11,3},{4,12},{12,4},... | collective-permute-start | bytes 43016 | tf_op jit(solution)/shard_map/ppermute | solution.py:190
  121.6 132.9 %collective-permute-start.5 = (f32[128,2048]{1,0:T(8,128)}, f32[128,2048]{1,0:T(8,128)}, u32[]{:S(2)}, u32[]{:S(2)}) collective-permute-start(f32[128,2048]{1,0:T(8,128)} %dynamic-slice_convert_fusion), channel_id=1, source_target_pairs={{0,8},{8,0},{1,9},{9,1},{2,10},{10,2},{3,11},{11,3},{4,12},{12,4},... | collective-permute-start | bytes 3145736 | tf_op jit(solution)/shard_map/ppermute | solution.py:190
  138.7 358.3 %collective-permute-start.7 = (f32[1536,1024]{1,0:T(8,128)}, f32[1536,1024]{1,0:T(8,128)}, u32[]{:S(2)}, u32[]{:S(2)}) collective-permute-start(f32[1536,1024]{1,0:T(8,128)} %fusion.42), channel_id=1, source_target_pairs={{0,8},{8,0},{1,9},{9,1},{2,10},{10,2},{3,11},{11,3},{4,12},{12,4},... | collective-permute-start | bytes 18874376 | tf_op jit(solution)/shard_map/ppermute | solution.py:190
  197.8 686.3 %collective-permute-start.9 = (f32[1536,1024]{1,0:T(8,128)}, f32[1536,1024]{1,0:T(8,128)}, u32[]{:S(2)}, u32[]{:S(2)}) collective-permute-start(f32[1536,1024]{1,0:T(8,128)} %fusion.41), channel_id=1, source_target_pairs={{0,8},{8,0},{1,9},{9,1},{2,10},{10,2},{3,11},{11,3},{4,12},{12,4},... | collective-permute-start | bytes 18874376 | tf_op jit(solution)/shard_map/ppermute | solution.py:190
  248.1 84.5 %copy-start.30 = (bf16[128,128]{1,0:T(8,128)(2,1)}, bf16[128,128]{1,0:T(8,128)(2,1)S(1)}, u32[]{:S(2)}) copy-start(bf16[128,128]{1,0:T(8,128)(2,1)S(1)} %add_convert_fusion.37.turn_ref) | copy-start | bytes 98308
  277.0 248.5 %copy-start.99 = (f32[1024]{0:T(1024)}, f32[1024]{0:T(1024)S(1)}, u32[]{:S(2)}) copy-start(f32[1024]{0:T(1024)S(1)} %convert_element_type.288) | copy-start | bytes 12292
  277.3 227.1 %copy-start.109 = (f32[1024]{0:T(1024)}, f32[1024]{0:T(1024)S(1)}, u32[]{:S(2)}) copy-start(f32[1024]{0:T(1024)S(1)} %convert_element_type.304) | copy-start | bytes 12292
  277.4 227.0 %copy-start.126 = (f32[1024]{0:T(1024)}, f32[1024]{0:T(1024)S(1)}, u32[]{:S(2)}) copy-start(f32[1024]{0:T(1024)S(1)} %convert_element_type.305) | copy-start | bytes 12292
  302.8 201.6 %copy-start.133 = (f32[4096]{0:T(1024)}, f32[4096]{0:T(1024)S(1)}, u32[]{:S(2)}) copy-start(f32[4096]{0:T(1024)S(1)} %pad_maximum_fusion.9) | copy-start | bytes 49156
  304.7 83.3 %copy-start.67 = (bf16[512,1024]{1,0:T(8,128)(2,1)}, bf16[512,1024]{1,0:T(8,128)(2,1)S(1)}, u32[]{:S(2)}) copy-start(bf16[512,1024]{1,0:T(8,128)(2,1)S(1)} %add_convert_fusion.30) | copy-start | bytes 3145732
  313.7 156.9 %copy-start.122 = (f32[1024]{0:T(1024)}, f32[1024]{0:T(1024)S(1)}, u32[]{:S(2)}) copy-start(f32[1024]{0:T(1024)S(1)} %broadcast_multiply_fusion.8) | copy-start | bytes 12292
  315.6 155.0 %copy-start.124 = (f32[1024]{0:T(1024)}, f32[1024]{0:T(1024)S(1)}, u32[]{:S(2)}) copy-start(f32[1024]{0:T(1024)S(1)} %add_rsqrt_fusion.2) | copy-start | bytes 12292
  572.7 253.5 %all-to-all-start = ((f32[8,1024,128]{2,1,0:T(8,128)}), f32[8,1024,128]{2,1,0:T(8,128)}, u32[]{:S(2)}, u32[]{:S(2)}) async-start(f32[8,1024,128]{2,1,0:T(8,128)} %bitcast_bitcast_fusion.2), calls=%async_computation | async-start | bytes 8388608 | tf_op jit(solution)/shard_map/all_to_all | solution.py:291
  577.5 140.2 %copy-start.25 = (f32[256,128]{1,0:T(8,128)S(1)}, f32[256,128]{1,0:T(8,128)}, u32[]{:S(2)}) copy-start(f32[256,128]{1,0:T(8,128)} %copy-done.24) | copy-start | bytes 393220
  577.6 140.2 %copy-start.28 = (f32[256,128]{1,0:T(8,128)S(1)}, f32[256,128]{1,0:T(8,128)}, u32[]{:S(2)}) copy-start(f32[256,128]{1,0:T(8,128)} %copy-done.27) | copy-start | bytes 393220
  577.6 140.2 %copy-start.31 = (bf16[128,128]{1,0:T(8,128)(2,1)S(1)}, bf16[128,128]{1,0:T(8,128)(2,1)}, u32[]{:S(2)}) copy-start(bf16[128,128]{1,0:T(8,128)(2,1)} %copy-done.30) | copy-start | bytes 98308
  577.6 250.7 %collective-permute-start.6 = (f32[1024,1024]{1,0:T(8,128)}, f32[1024,1024]{1,0:T(8,128)}, u32[]{:S(2)}, u32[]{:S(2)}) collective-permute-start(f32[1024,1024]{1,0:T(8,128)} %add_add_fusion.7), channel_id=1, source_target_pairs={{0,8},{8,0},{1,9},{9,1},{2,10},{10,2},{3,11},{11,3},{4,12},{12,4},... | collective-permute-start | bytes 12582920 | tf_op jit(solution)/shard_map/ppermute | solution.py:190
  693.6 105.1 %slice-start.2 = ((s8[6291456]{0:T(1024)(128)(4,1)}), s8[4194304]{0:T(1024)(128)(4,1)S(1)}, s32[]{:S(2)}) async-start(s8[6291456]{0:T(1024)(128)(4,1)} %bitcast.214), calls=%async_computation.21 | async-start | bytes 8388608
  818.9 423.3 %collective-permute-start.8 = (f32[1536,1024]{1,0:T(8,128)}, f32[1536,1024]{1,0:T(8,128)}, u32[]{:S(2)}, u32[]{:S(2)}) collective-permute-start(f32[1536,1024]{1,0:T(8,128)} %add_add_fusion.3), channel_id=1, source_target_pairs={{0,8},{8,0},{1,9},{9,1},{2,10},{10,2},{3,11},{11,3},{4,12},{12,4},... | collective-permute-start | bytes 18874376 | tf_op jit(solution)/shard_map/ppermute | solution.py:190
  826.3 220.1 %collective-permute-start.10 = (f32[8,1024,128]{2,1,0:T(8,128)}, f32[8,1024,128]{2,1,0:T(8,128)}, u32[]{:S(2)}, u32[]{:S(2)}) collective-permute-start(f32[8,1024,128]{2,1,0:T(8,128)} %all-to-all-done), channel_id=1, source_target_pairs={{0,8},{8,0},{1,9},{9,1},{2,10},{10,2},{3,11},{11,3},{4,12},{12,4},... | collective-permute-start | bytes 12582920 | tf_op jit(solution)/shard_map/ppermute | solution.py:190
  879.0 167.4 %copy-start.47 = (bf16[1536,1024]{1,0:T(8,128)(2,1)S(1)}, bf16[1536,1024]{1,0:T(8,128)(2,1)}, u32[]{:S(2)}) copy-start(bf16[1536,1024]{1,0:T(8,128)(2,1)} %gather_fusion.4) | copy-start | bytes 9437188
  879.0 167.4 %copy-start.137 = (pred[1536]{0:T(1024)(128)(4,1)S(1)}, pred[1536]{0:T(1024)(128)(4,1)}, u32[]{:S(2)}) copy-start(pred[1536]{0:T(1024)(128)(4,1)} %get-tuple-element.205) | copy-start | bytes 4612
  879.0 167.4 %copy-start.138 = (pred[1536]{0:T(1024)(128)(4,1)S(1)}, pred[1536]{0:T(1024)(128)(4,1)}, u32[]{:S(2)}) copy-start(pred[1536]{0:T(1024)(128)(4,1)} %get-tuple-element.206) | copy-start | bytes 4612
  879.0 363.2 %all-to-all-start.1 = ((f32[8,1536,128]{2,1,0:T(8,128)}), f32[8,1536,128]{2,1,0:T(8,128)}, u32[]{:S(2)}, u32[]{:S(2)}) async-start(f32[8,1536,128]{2,1,0:T(8,128)} %bitcast.217), calls=%async_computation.1 | async-start | bytes 12582912 | tf_op jit(solution)/shard_map/all_to_all | solution.py:291
  884.1 907.6 %reduce-scatter.13.cloned.1.call-start = ((), (), s32[]{:S(2)}) async-start(), calls=%async_computation.16 | async-start | bytes 4718592 | tf_op jit(solution)/shard_map/reduce_scatter | solution.py:313
  1301.7 493.1 %reduce-scatter.7.cloned.1.call-start = ((), (), s32[]{:S(2)}) async-start(), calls=%async_computation.13 | async-start | bytes 4718592 | tf_op jit(solution)/shard_map/reduce_scatter | solution.py:313
  1317.2 478.6 %reduce-scatter.9.cloned.1.call-start = ((), (), s32[]{:S(2)}) async-start(), calls=%async_computation.14 | async-start | bytes 4718592 | tf_op jit(solution)/shard_map/reduce_scatter | solution.py:313
  1332.7 464.2 %reduce-scatter.11.cloned.1.call-start = ((), (), s32[]{:S(2)}) async-start(), calls=%async_computation.15 | async-start | bytes 4718592 | tf_op jit(solution)/shard_map/reduce_scatter | solution.py:313
  1368.2 583.6 %reduce-scatter.17.cloned.1.call-start = ((), (), s32[]{:S(2)}) async-start(), calls=%async_computation.18 | async-start | bytes 18874368 | tf_op jit(solution)/shard_map/reduce_scatter | solution.py:313
  1416.1 136.9 %collective-permute-start.11 = (f32[1536,1024]{1,0:T(8,128)}, f32[1536,1024]{1,0:T(8,128)}, u32[]{:S(2)}, u32[]{:S(2)}) collective-permute-start(f32[1536,1024]{1,0:T(8,128)} %add_add_fusion.2), channel_id=1, source_target_pairs={{0,8},{8,0},{1,9},{9,1},{2,10},{10,2},{3,11},{11,3},{4,12},{12,4},... | collective-permute-start | bytes 18874376 | tf_op jit(solution)/shard_map/ppermute | solution.py:190
  1416.5 136.5 %all-to-all-start.2 = ((f32[8,1536,128]{2,1,0:T(8,128)}), f32[8,1536,128]{2,1,0:T(8,128)}, u32[]{:S(2)}, u32[]{:S(2)}) async-start(f32[8,1536,128]{2,1,0:T(8,128)} %bitcast.216), calls=%async_computation.2 | async-start | bytes 12582912 | tf_op jit(solution)/shard_map/all_to_all | solution.py:291
  1421.3 537.5 %reduce-scatter.15.cloned.1.call-start = ((), (), s32[]{:S(2)}) async-start(), calls=%async_computation.17 | async-start | bytes 18874368 | tf_op jit(solution)/shard_map/reduce_scatter | solution.py:313
  1633.4 165.3 %collective-permute-start.13 = (f32[8,1536,128]{2,1,0:T(8,128)}, f32[8,1536,128]{2,1,0:T(8,128)}, u32[]{:S(2)}, u32[]{:S(2)}) collective-permute-start(f32[8,1536,128]{2,1,0:T(8,128)} %all-to-all-done.1), channel_id=1, source_target_pairs={{0,8},{8,0},{1,9},{9,1},{2,10},{10,2},{3,11},{11,3},{4,12},{12,4},... | collective-permute-start | bytes 18874376 | tf_op jit(solution)/shard_map/ppermute | solution.py:190
  1661.5 109.8 %collective-permute-start.14 = (f32[1088]{0:T(1024)S(1)}, f32[1088]{0:T(1024)S(1)}, u32[]{:S(2)}, u32[]{:S(2)}) collective-permute-start(f32[1088]{0:T(1024)S(1)} %pad_maximum_fusion.10), channel_id=1, source_target_pairs={{0,8},{8,0},{1,9},{9,1},{2,10},{10,2},{3,11},{11,3},{4,12},{12,4},... | collective-permute-start | bytes 13064 | tf_op jit(solution)/shard_map/ppermute | solution.py:190
  1791.0 169.1 %collective-permute-start.12 = (f32[8,1536,128]{2,1,0:T(8,128)}, f32[8,1536,128]{2,1,0:T(8,128)}, u32[]{:S(2)}, u32[]{:S(2)}) collective-permute-start(f32[8,1536,128]{2,1,0:T(8,128)} %all-to-all-done.2), channel_id=1, source_target_pairs={{0,8},{8,0},{1,9},{9,1},{2,10},{10,2},{3,11},{11,3},{4,12},{12,4},... | collective-permute-start | bytes 18874376 | tf_op jit(solution)/shard_map/ppermute | solution.py:190
  1793.3 141.7 %collective-permute-start.16 = (f32[512,128]{1,0:T(8,128)}, f32[512,128]{1,0:T(8,128)}, u32[]{:S(2)}, u32[]{:S(2)}) collective-permute-start(f32[512,128]{1,0:T(8,128)} %slice.313), channel_id=1, source_target_pairs={{0,8},{8,0},{1,9},{9,1},{2,10},{10,2},{3,11},{11,3},{4,12},{12,4},... | collective-permute-start | bytes 786440 | tf_op jit(solution)/shard_map/ppermute | solution.py:190
  1798.0 152.5 %collective-permute-start.15 = (f32[3,128,512]{2,1,0:T(8,128)S(1)}, f32[3,128,512]{2,1,0:T(8,128)S(1)}, u32[]{:S(2)}, u32[]{:S(2)}) collective-permute-start(f32[3,128,512]{2,1,0:T(8,128)S(1)} %pad_maximum_fusion.6), channel_id=1, source_target_pairs={{0,8},{8,0},{1,9},{9,1},{2,10},{10,2},{3,11},{11,3},{4,12},{12,4},... | collective-permute-start | bytes 2359304 | tf_op jit(solution)/shard_map/ppermute | solution.py:190
  1798.7 136.4 %copy-start.97 = (f32[1024,128]{1,0:T(8,128)S(1)}, f32[1024,128]{1,0:T(8,128)}, u32[]{:S(2)}) copy-start(f32[1024,128]{1,0:T(8,128)} %reduce-scatter.13.cloned.1.call-done) | copy-start | bytes 1572868
  1953.1 79.9 %collective-permute-start.18 = (f32[2048,128]{1,0:T(8,128)S(1)}, f32[2048,128]{1,0:T(8,128)S(1)}, u32[]{:S(2)}, u32[]{:S(2)}) collective-permute-start(f32[2048,128]{1,0:T(8,128)S(1)} %slice.317), channel_id=1, source_target_pairs={{0,8},{8,0},{1,9},{9,1},{2,10},{10,2},{3,11},{11,3},{4,12},{12,4},... | collective-permute-start | bytes 3145736 | tf_op jit(solution)/shard_map/ppermute | solution.py:190
  1960.0 74.1 %collective-permute-start.17 = (f32[128,2048]{1,0:T(8,128)S(1)}, f32[128,2048]{1,0:T(8,128)S(1)}, u32[]{:S(2)}, u32[]{:S(2)}) collective-permute-start(f32[128,2048]{1,0:T(8,128)S(1)} %slice.315), channel_id=1, source_target_pairs={{0,8},{8,0},{1,9},{9,1},{2,10},{10,2},{3,11},{11,3},{4,12},{12,4},... | collective-permute-start | bytes 3145736 | tf_op jit(solution)/shard_map/ppermute | solution.py:190
  (165 other events, 2317.7 us)
Sparse Core Ops, SparseCore 0:
  18.7 25.0 all-gather.7
  46.1 41.2 all-gather.5
  89.2 50.1 all-gather.9
  254.6 48.7 all-gather.11
  1301.8 45.3 reduce-scatter.12
  1350.4 45.1 reduce-scatter.6
  1398.9 78.5 reduce-scatter.8
  1480.8 58.3 reduce-scatter.10
  1542.7 111.5 reduce-scatter.16
  1657.7 109.6 reduce-scatter.14

commit v2 on v1

--- a/solution.py
+++ b/solution.py
@@ -6,9 +6,11 @@
 from jax.experimental.pallas import tpu as pltpu
 from jax.sharding import PartitionSpec as P
 
+
 EPS_NORM = 1e-5
 ROPE_BASE = 10000.0
 CHUNKS = (4, 6, 6)
+SPILL = 64
 HALF_ROOT = 0.5 ** 0.5
 PDF_SCALE = (2.0 * 3.141592653589793) ** -0.5
 F32, BF16 = jnp.float32, jnp.bfloat16
@@ -34,8 +36,8 @@
     return jnp.tile(cos_head, (1, 2)), jnp.tile(sin_head, (1, 2)), turn.astype(BF16)
 
 
-def attention_kernel(head_dim, q_ref, k_ref, v_ref, g_ref, cos_ref, sin_ref, turn_ref, ctx_ref, dq_ref, dk_ref, dv_ref):
-    seq_len, width = q_ref.shape[1], q_ref.shape[2]
+def attention_kernel(head_dim, qkv_ref, g_ref, cos_ref, sin_ref, turn_ref, ctx_ref, dqkv_ref):
+    seq_len, width = g_ref.shape[1], g_ref.shape[2]
     pair = 2 * head_dim
     scale = head_dim ** -0.5
     cos, sin, turn = cos_ref[...], sin_ref[...], turn_ref[...]
@@ -52,9 +54,11 @@
 
     def step(j, carry):
         cols = pl.ds(pl.multiple_of(j * pair, pair), pair)
-        q = rotate(q_ref[0, :, cols])
-        k = rotate(k_ref[0, :, cols])
-        v = v_ref[0, :, cols]
+        k_cols = pl.ds(pl.multiple_of(width + j * pair, pair), pair)
+        v_cols = pl.ds(pl.multiple_of(2 * width + j * pair, pair), pair)
+        q = rotate(qkv_ref[0, :, cols])
+        k = rotate(qkv_ref[0, :, k_cols])
+        v = qkv_ref[0, :, v_cols]
         g = g_ref[0, :, cols]
         parts = []
         for head in range(2):
@@ -77,30 +81,29 @@
             parts.append((ctx, d_q, d_k, d_v))
         ctx, d_q, d_k, d_v = (jnp.where(low, a, b).astype(BF16) for a, b in zip(*parts))
         ctx_ref[0, :, cols] = ctx
-        dq_ref[0, :, cols] = unrotate(d_q)
-        dk_ref[0, :, cols] = unrotate(d_k)
-        dv_ref[0, :, cols] = d_v
+        dqkv_ref[0, :, cols] = unrotate(d_q)
+        dqkv_ref[0, :, k_cols] = unrotate(d_k)
+        dqkv_ref[0, :, v_cols] = d_v
         return carry
 
     lax.fori_loop(0, width // pair, step, 0)
 
 
-def attention(q, k, v, g, consts, head_dim):
-    n, seq_len, width = q.shape
-    big = pl.BlockSpec((1, seq_len, width), lambda i: (i, 0, 0))
+def attention(qkv, g, consts, head_dim):
+    n, seq_len, width = g.shape
+    big = lambda w: pl.BlockSpec((1, seq_len, w), lambda i: (i, 0, 0))
     const = [pl.BlockSpec(c.shape, lambda i: (0, 0)) for c in consts]
-    shape = jax.ShapeDtypeStruct(q.shape, BF16)
     flops = n * (width // head_dim) * 12 * seq_len * seq_len * 2 * head_dim
     return pl.pallas_call(
         functools.partial(attention_kernel, head_dim),
         grid=(n,),
-        in_specs=[big] * 4 + const,
-        out_specs=[big] * 4,
-        out_shape=[shape] * 4,
+        in_specs=[big(3 * width), big(width)] + const,
+        out_specs=[big(width), big(3 * width)],
+        out_shape=[jax.ShapeDtypeStruct(g.shape, BF16), jax.ShapeDtypeStruct(qkv.shape, BF16)],
         compiler_params=pltpu.CompilerParams(dimension_semantics=("arbitrary",), vmem_limit_bytes=40 * 1024 * 1024),
-        cost_estimate=pl.CostEstimate(flops=4 * flops, bytes_accessed=16 * q.size, transcendentals=0),
+        cost_estimate=pl.CostEstimate(flops=4 * flops, bytes_accessed=16 * g.size, transcendentals=0),
         name="attention",
-    )(q, k, v, g, *consts)
+    )(qkv, g, *consts)
 
 
 def scatter_kernel(has_init, rows, block, counts, *refs):
@@ -122,6 +125,7 @@
             if not has_init:
                 acc0[at, :] = jnp.zeros((8, acc0.shape[1]), F32)
             return carry
+
         lax.fori_loop(0, padded // 8, clear, 0, unroll=8)
         if has_init:
             copy = pltpu.make_async_copy(init_ref, acc0.at[pl.ds(0, rows)], sem)
@@ -139,7 +143,9 @@
                     acc0[pl.ds(r0, 1), :] += g_ref[pl.ds(at, 1), :]
                     acc1[pl.ds(r1, 1), :] += g_ref[pl.ds(at + 1, 1), :]
                 return carry
+
             lax.fori_loop(0, block // group, add_group, 0)
+
         pl.when((step >= first) & (step < first + count))(add_block)
         first += count
 
@@ -149,6 +155,7 @@
             at = pl.ds(pl.multiple_of(i * 8, 8), 8)
             acc0[at, :] += acc1[at, :]
             return carry
+
         lax.fori_loop(0, padded // 8, merge, 0, unroll=8)
         copy = pltpu.make_async_copy(acc0.at[pl.ds(0, rows)], out_ref, sem)
         copy.start()
@@ -174,7 +181,7 @@
         in_specs=in_specs,
         out_specs=pl.BlockSpec(memory_space=pl.ANY),
         out_shape=jax.ShapeDtypeStruct((rows, width), F32),
-        scratch_shapes=[pltpu.VMEM((rows + 8, width), F32), pltpu.VMEM((rows + 8, width), F32), pltpu.SemaphoreType.DMA],
+        scratch_shapes=[pltpu.VMEM((rows + SPILL, width), F32), pltpu.VMEM((rows + SPILL, width), F32), pltpu.SemaphoreType.DMA],
         compiler_params=pltpu.CompilerParams(dimension_semantics=("arbitrary",), vmem_limit_bytes=40 * 1024 * 1024),
         cost_estimate=pl.CostEstimate(flops=total * block * 3000000, bytes_accessed=8 * total * block * width, transcendentals=0),
         name="scatter_rows",
@@ -203,13 +210,15 @@
         def from_peer(w):
             size = w.shape[0] // n_dp
             piece = swap(lax.dynamic_slice_in_dim(w, dp_i * size, size, 0).astype(F32))
+            piece, _ = lax.optimization_barrier((piece, first_rows))
             whole = lax.all_gather(piece, 'dp', axis=0, tiled=True)
             return (whole + zero).astype(BF16)
 
         def rows_of(ids):
             local = ids - tp_i * vocab_local
             ok = (local >= 0) & (local < vocab_local)
-            picked = jnp.take(embed_table, jnp.where(ok, local, 0), axis=0)
+            other = jnp.where(local < 0, local + vocab_local, local - vocab_local)
+            picked = jnp.take(embed_table, jnp.where(ok, local, other), axis=0, mode='clip')
             return jnp.where(ok[..., None], picked, jnp.zeros_like(picked)).astype(F32)
 
         ids_own = lax.dynamic_slice_in_dim(token_ids, own_at, half_seq, 0)
@@ -219,19 +228,20 @@
         for size in CHUNKS:
             bounds.append((start, start + size))
             start += size
-        sent_x = [swap(rows_of(ids_peer[a:b].reshape(-1))) for a, b in bounds]
+        first_rows = rows_of(ids_peer[bounds[0][0]:bounds[0][1]].reshape(-1))
+        sent_x = [swap(first_rows)] + [swap(rows_of(ids_peer[a:b].reshape(-1))) for a, b in bounds[1:]]
 
         wqkv_own = w_qkv.transpose(2, 0, 1, 3).reshape(3 * d_model, attn_local)
         wqkv_peer = from_peer(wqkv_own)
-        w_q, w_k, w_v = (jnp.concatenate([wqkv_own[i * d_model:(i + 1) * d_model], wqkv_peer[i * d_model:(i + 1) * d_model]], axis=1) for i in range(3))
-        fc2_all = jnp.concatenate([w_fc2, from_peer(w_fc2)], axis=0)
+        qkv_all = jnp.concatenate([w[i * d_model:(i + 1) * d_model] for i in range(3) for w in (wqkv_own, wqkv_peer)], axis=1)
         dense_own = w_dense.reshape(attn_local, d_model)
         dense_all = jnp.concatenate([dense_own, from_peer(dense_own)], axis=0)
         fc1_all = jnp.concatenate([w_fc1, from_peer(w_fc1)], axis=1)
+        fc2_all = jnp.concatenate([w_fc2, from_peer(w_fc2)], axis=0)
         bqkv_own = b_qkv.transpose(1, 0, 2).reshape(-1)
         bias_own = jnp.concatenate([bqkv_own, b_fc1]).astype(F32)
         bias_peer = swap(bias_own)
-        b_q, b_k, b_v = (jnp.concatenate([bias_own[i * attn_local:(i + 1) * attn_local], bias_peer[i * attn_local:(i + 1) * attn_local]]) for i in range(3))
+        bqkv_all = jnp.concatenate([v[i * attn_local:(i + 1) * attn_local] for i in range(3) for v in (bias_own, bias_peer)])
         bfc1_all = jnp.concatenate([bias_own[3 * attn_local:], bias_peer[3 * attn_local:]])
 
         gain1, gain2 = ln1_gain.astype(F32), ln2_gain.astype(F32)
@@ -240,23 +250,26 @@
         consts = rope_consts(seq_len, head_dim)
         ids_all = lax.all_gather(token_ids, 'dp', axis=0)
         local_all = ids_all - tp_i * vocab_local
-        local_all = jnp.where((local_all >= 0) & (local_all < vocab_local), local_all, vocab_local)
+        spread = vocab_local + lax.broadcasted_iota(jnp.int32, local_all.shape, 2) % SPILL
+        local_all = jnp.where((local_all >= 0) & (local_all < vocab_local), local_all, spread)
         local_own = lax.dynamic_slice_in_dim(local_all, own_at, half_seq, 1)
         local_peer = lax.dynamic_slice_in_dim(local_all, peer_at, half_seq, 1)
         cot_own = lax.dynamic_slice_in_dim(cotangent, own_at, half_seq, 0)
 
         layer_out = jnp.zeros(cotangent.shape, BF16)
         scatter_parts = []
-        dw_sum = None
-        after, held, older = None, [], []
-        small_sum = None
+        dw_sum = small_sum = None
+        t0 = ((0,), (0,))
+        total = lambda v: jnp.sum(v.astype(F32), axis=0)
+        after, held, older = [], [], []
         for (a, b), recv_x in zip(bounds, sent_x):
+            last = b == half_seq
             tokens = (b - a) * seq_len
             flat = lambda v: v.reshape(tokens, v.shape[-1])
+            cube = lambda v: v.reshape(b - a, seq_len, v.shape[-1])
             cot = flat(cot_own[a:b])
-            if after is not None:
-                cot, recv_x, _ = lax.optimization_barrier((cot, recv_x, after + older))
-                older = late
+            if after:
+                cot, recv_x, _ = lax.optimization_barrier((cot, recv_x, after))
             grad_act = dot_f32(cot, fc2_all, ((1,), (1,))).astype(BF16)
             grad_ctx = dot_f32(cot, dense_all, ((1,), (1,))).astype(BF16)
             x = rows_of(ids_own[a:b].reshape(-1)) + recv_x
@@ -265,10 +278,10 @@
             normed = centered * inv_std
             hid1 = (normed * gain1 + shift1).astype(BF16)
             hid2 = (normed * gain2 + shift2).astype(BF16)
-            q, k, v = ((dot_f32(hid1, w, ((1,), (0,))) + bias).astype(BF16).reshape(b - a, seq_len, -1) for w, bias in ((w_q, b_q), (w_k, b_k), (w_v, b_v)))
-            ctx, d_q, d_k, d_v = (flat(r) for r in attention(q, k, v, grad_ctx.reshape(b - a, seq_len, -1), consts, head_dim))
+            qkv = (dot_f32(hid1, qkv_all, ((1,), (0,))) + bqkv_all).astype(BF16)
             pre_low = (dot_f32(hid2, fc1_all, ((1,), (0,))) + bfc1_all).astype(BF16)
             grad_act, pre_low = lax.optimization_barrier((grad_act, pre_low))
+            ctx, d_qkv = (flat(r) for r in attention(cube(qkv), cube(grad_ctx), consts, head_dim))
             pre_act = pre_low.astype(F32)
             cdf = 0.5 + 0.5 * lax.erf(pre_act * HALF_ROOT)
             act = (pre_act * cdf).astype(BF16)
@@ -276,64 +289,68 @@
             grad_pre = (grad_act.astype(F32) * slope).astype(BF16)
             out_sum = x + dot_f32(ctx, dense_all, ((1,), (0,))) + dot_f32(act, fc2_all, ((1,), (0,)))
             recv_out = swap(out_sum)
-            as_out = lambda v: (v + out_bias).astype(BF16).reshape(b - a, seq_len, d_model)
-            layer_out = lax.dynamic_update_slice_in_dim(layer_out, as_out(out_sum), own_at + a, 0)
-            layer_out = lax.dynamic_update_slice_in_dim(layer_out, as_out(recv_out), peer_at + a, 0)
-
-            if held:
-                out_sum, act, grad_pre, d_q, d_k, d_v, _ = lax.optimization_barrier((out_sum, act, grad_pre, d_q, d_k, d_v, held))
-                held = []
+            d_fc2, d_dense = dot_f32(act, cot, t0), dot_f32(ctx, cot, t0)
+            if dw_sum is not None:
+                d_fc2, d_dense = dw_sum[0] + d_fc2, dw_sum[1] + d_dense
+            grad_pre, d_qkv, _ = lax.optimization_barrier((grad_pre, d_qkv, [out_sum, d_fc2, d_dense] + held))
+
             grad_h2 = dot_f32(grad_pre, fc1_all, ((1,), (1,))).astype(BF16).astype(F32)
-            grad_h1 = (dot_f32(d_q, w_q, ((1,), (1,))) + dot_f32(d_k, w_k, ((1,), (1,))) + dot_f32(d_v, w_v, ((1,), (1,)))).astype(BF16).astype(F32)
+            grad_h1 = dot_f32(d_qkv, qkv_all, ((1,), (1,))).astype(BF16).astype(F32)
             grad_norm = grad_h1 * gain1 + grad_h2 * gain2
             grad_x = cot.astype(F32) + inv_std * (grad_norm - jnp.mean(grad_norm, axis=-1, keepdims=True) - normed * jnp.mean(grad_norm * normed, axis=-1, keepdims=True))
             by_col = grad_x.reshape(tokens, n_dp, d_model // n_dp).transpose(1, 0, 2)
             mine = lax.all_to_all(by_col, 'dp', split_axis=0, concat_axis=0, tiled=True)
             theirs = swap(mine)
-            after, held, late = [by_col, out_sum], [mine, recv_out], [theirs]
             scatter_parts.append((local_own[:, a:b].reshape(-1), mine.reshape(-1, d_model // n_dp), local_peer[:, a:b].reshape(-1), theirs.reshape(-1, d_model // n_dp)))
 
-            if b == half_seq:
-                hid1, hid2, ctx, act, grad_pre, d_q, d_k, d_v, _ = lax.optimization_barrier((hid1, hid2, ctx, act, grad_pre, d_q, d_k, d_v, by_col))
-            t0 = ((0,), (0,))
-            hid_fc1, pre_fc1 = hid2, grad_pre
-            if b == half_seq:
-                hid_fc1, pre_fc1, _ = lax.optimization_barrier((hid2, grad_pre, [mine, recv_out]))
-            dws = [dot_f32(hid1, d_q, t0), dot_f32(hid1, d_k, t0), dot_f32(hid1, d_v, t0), dot_f32(ctx, cot, t0), dot_f32(hid_fc1, pre_fc1, t0), dot_f32(act, cot, t0)]
-            total = lambda v: jnp.sum(v.astype(F32), axis=0)
-            smalls = [total(grad_h1 * normed), total(grad_h1), total(grad_h2 * normed), total(grad_h2), total(cot), total(d_q), total(d_k), total(d_v), total(grad_pre)]
-            dw_sum = dws if dw_sum is None else [p + r for p, r in zip(dw_sum, dws)]
+            hid1, hid2, grad_pre, d_qkv, _ = lax.optimization_barrier((hid1, hid2, grad_pre, d_qkv, by_col))
+            d_fc1 = dot_f32(hid2, grad_pre, t0)
+            d_wqkv = dot_f32(hid1, d_qkv, t0)
+            if dw_sum is not None:
+                d_fc1, d_wqkv = dw_sum[2] + d_fc1, dw_sum[3] + d_wqkv
+            dw_sum = [d_fc2, d_dense, d_fc1, d_wqkv]
+            smalls = [total(grad_h1 * normed), total(grad_h1), total(grad_h2 * normed), total(grad_h2), total(cot), total(d_qkv), total(grad_pre)]
             small_sum = smalls if small_sum is None else [p + r for p, r in zip(small_sum, smalls)]
+            after = [by_col, d_fc1, d_wqkv] + small_sum
+            held, older = [mine] + older, [recv_out, theirs]
+            as_out = lambda v: (v + out_bias).astype(BF16).reshape(b - a, seq_len, d_model)
+            layer_out = lax.dynamic_update_slice_in_dim(layer_out, as_out(out_sum), own_at + a, 0)
+            if last:
+                last_out = (recv_out, a, as_out)
+            else:
+                layer_out = lax.dynamic_update_slice_in_dim(layer_out, as_out(recv_out), peer_at + a, 0)
 
         pick = lambda parts, i: [p for part in parts for p in (part[i], part[i + 2])]
         embed_first = scatter_rows(pick(scatter_parts[:-1], 0), pick(scatter_parts[:-1], 1), vocab_local)
         sum_embed = scatter_rows(pick(scatter_parts[-1:], 0), pick(scatter_parts[-1:], 1), vocab_local, embed_first)
-
-        d_wq, d_wk, d_wv, d_dense, d_fc1, d_fc2 = dw_sum
+        recv_out, a, as_out = last_out
+        recv_out, _ = lax.optimization_barrier((recv_out, embed_first[:8]))
+        layer_out = lax.dynamic_update_slice_in_dim(layer_out, as_out(recv_out), peer_at + a, 0)
+
+        d_fc2, d_dense, d_fc1, d_wqkv = dw_sum
         rs = lambda v, dim: lax.psum_scatter(v, 'dp', scatter_dimension=dim, tiled=True)
-        r_fc2, r_fc1, r_dense = rs(d_fc2, 1), rs(d_fc1, 0), rs(d_dense, 1)
-        r_q, r_k, r_v = rs(d_wq, 0), rs(d_wk, 0), rs(d_wv, 0)
-        sum_fc2 = r_fc2[:ff_local] + swap(r_fc2[ff_local:])
-        sum_fc1 = r_fc1[:, :ff_local] + swap(r_fc1[:, ff_local:])
-        sum_dense = (r_dense[:attn_local] + swap(r_dense[attn_local:])).reshape(heads_local, head_dim, -1)
-        own_qkv = jnp.stack([r[:, :attn_local].reshape(-1, heads_local, head_dim) for r in (r_q, r_k, r_v)], axis=2)
-        peer_qkv = jnp.stack([r[:, attn_local:] for r in (r_q, r_k, r_v)])
-        got_qkv = swap(peer_qkv).reshape(3, -1, heads_local, head_dim).transpose(1, 2, 0, 3)
-        sum_qkv = own_qkv + got_qkv
-
-        s_bqkv = [v.reshape(2, heads_local, head_dim) for v in small_sum[5:8]]
-        bqkv_grad = jnp.stack(s_bqkv, axis=2)
-        fc1_bias = small_sum[8].reshape(2, -1)
-        pieces = small_sum[:5] + [bqkv_grad[0].reshape(-1), fc1_bias[0], bqkv_grad[1].reshape(-1), fc1_bias[1]]
-        packed = jnp.concatenate([p.reshape(n_dp, -1) for p in pieces], axis=1)
-        got = rs(packed, 0)[0]
-        n_common = 5 * d_model // n_dp
-        n_side = (3 * attn_local + ff_local) // n_dp
-        common, side_own, side_peer = got[:n_common], got[n_common:n_common + n_side], got[n_common + n_side:]
-        moved = swap(jnp.concatenate([common, side_peer]))
-        common = (common + moved[:n_common]).reshape(5, -1)
-        side = side_own + moved[n_common:]
-        sum_bqkv, sum_bfc1 = side[:3 * attn_local // n_dp], side[3 * attn_local // n_dp:]
+        r_fc2 = rs(d_fc2, 1)
+        r_dense = rs(d_dense, 1)
+        r_fc1 = rs(d_fc1, 0)
+        r_qkv = rs(d_wqkv, 0)
+        r_qkv = r_qkv.reshape(-1, 3, 2, heads_local, head_dim)
+        got = [swap(r_fc2[ff_local:]), swap(r_dense[attn_local:]), swap(r_fc1[:, ff_local:]), swap(r_qkv[:, :, 1].reshape(-1, 3 * attn_local))]
+        got, _ = lax.optimization_barrier((got, sum_embed[:8]))
+        sum_fc2 = r_fc2[:ff_local] + got[0]
+        sum_dense = (r_dense[:attn_local] + got[1]).reshape(heads_local, head_dim, -1)
+        sum_fc1 = r_fc1[:, :ff_local] + got[2]
+        sum_qkv = (r_qkv[:, :, 0] + got[3].reshape(-1, 3, heads_local, head_dim)).transpose(0, 2, 1, 3)
+
+        bqkv_grad = small_sum[5].reshape(3, 2, heads_local, head_dim).transpose(1, 2, 0, 3).reshape(2, -1)
+        side = jnp.concatenate([bqkv_grad, small_sum[6].reshape(2, -1)], axis=1)
+        side = jnp.where(tp_i == 0, side, side[::-1])
+        packed = lax.psum(jnp.concatenate(small_sum[:5] + [side[0], side[1]]), ('tp', 'dp'))
+        piece = d_model // n_dp
+        common = [lax.dynamic_slice_in_dim(packed, i * d_model + dp_i * piece, piece, 0) for i in range(5)]
+        base = 5 * d_model + tp_i * side.shape[1]
+        n_b, n_f = 3 * attn_local // n_dp, ff_local // n_dp
+        sum_bqkv = lax.dynamic_slice_in_dim(packed, base + dp_i * n_b, n_b, 0)
+        sum_bfc1 = lax.dynamic_slice_in_dim(packed, base + 3 * attn_local + dp_i * n_f, n_f, 0)
         return (layer_out, sum_embed, common[0], common[1], common[2], common[3], sum_qkv, sum_bqkv, sum_dense, common[4], sum_fc1, sum_bfc1, sum_fc2, common[4])
 
     return jax.shard_map(device_step, mesh=mesh, in_specs=arg_specs, out_specs=out_specs, check_vma=False)

time: 2080 us -> 1970 us (0.947); the launches traced: 2040 us -> 1960 us
  blocking collectives: 35.2 us -> 397 us
  waiting for transfers between devices: 453 us -> 188 us
  starting transfers between devices: 272 us -> 35.2 us
  other arithmetic: 175 us -> 216 us
    psum x0 -> x1, blocking collectives: none -> 386 us  [device_step(): lax.psum(jnp.concatenate(small_sum[:5] + [side[0], side[1]]), ('tp', 'dp'))]
    ppermute x19 -> x18, waiting for transfers between devices: 453 us -> 187 us  [swap(): return lax.ppermute(val, 'tp', [(0, 1), (1, 0)])]
    ppermute x19 -> x18, starting transfers between devices: 256 us -> 19.4 us  [swap(): return lax.ppermute(val, 'tp', [(0, 1), (1, 0)])]
    unnamed x1 -> x0, blocking collectives: 25 us -> none
    convert_element_type x2 -> x3, other arithmetic: 40.1 us -> 61.7 us  [device_step(): grad_pre = (grad_act.astype(F32) * slope).astype(BF16)]
    dot_general x54 -> x36, matrix products: 547 us -> 562 us  [dot_f32(): return lax.dot_general(a, b, (dims, ((), ())), preferred_element_type=F32)]
    reduce_sum x15 -> x9, other arithmetic: 59 us -> 49.8 us  [device_step(): total = lambda v: jnp.sum(v.astype(F32), axis=0)]
  transfers between devices with their start and end apart: 32 -> 29, of which waited for: 8 -> 5; matrix products, arithmetic and copies ran while one was open for 39% -> 47% of each run, Pallas kernels for 18% -> 19%
where the time goes in v2:
time: 1970 us; the launch traced here: 1960 us
  matrix products  562 us (29%)
  blocking collectives  397 us (20%)
  Pallas kernels  380 us (19%)
  other arithmetic  216 us (11%)
  waiting for transfers between devices  188 us (10%)
  local copies, waits for them, and re-layouts  162 us (8%)
  starting transfers between devices  35.2 us (2%)
    dot_general x36, matrix products, dot_f32(): return lax.dot_general(a, b, (dims, ((), ())), preferred_element_type=F32)  562 us
    psum x1, blocking collectives, device_step(): lax.psum(jnp.concatenate(small_sum[:5] + [side[0], side[1]]), ('tp', 'dp'))  386 us
    pallas_call x3, Pallas kernels, attention(): pl.pallas_call(functools.partial(attention_kernel, head_dim), grid=(n,),...  205 us
    ppermute x18, waiting for transfers between devices, swap(): return lax.ppermute(val, 'tp', [(0, 1), (1, 0)])  187 us
    pallas_call x2, Pallas kernels, scatter_rows(): pl.pallas_call(functools.partial(scatter_kernel, has_init, rows, block, c...  175 us
    gather x6, local copies, waits for them, and re-layouts, rows_of(): jnp.take(embed_table, jnp.where(ok, local, other), axis=0, mode='clip')  89.8 us
    convert_element_type x3, other arithmetic, device_step(): grad_pre = (grad_act.astype(F32) * slope).astype(BF16)  61.7 us
    reduce_sum x9, other arithmetic, device_step(): total = lambda v: jnp.sum(v.astype(F32), axis=0)  49.8 us
  transfers between devices with their start and end apart: 29, of which 5 were waited for; matrix products, arithmetic and copies ran while one was open for 47% of the time, Pallas kernels for 19%

profile of v2, /device:TPU:0, one launch (start us, length us, event | category | flops | bytes accessed | tf_op | source)
XLA Modules:
  0.0 1957.2 jit_solution(15718313215988060262)
XLA Ops:
  13.0 20.1 %gather_fusion.1 = bf16[1024,1024]{1,0:T(8,128)(2,1)} fusion(bf16[25152,1024]{1,0:T(8,128)(2,1)} %param.16, s32[1024]{0:T(1024)S(1)} %broadcast_clamp_fusion), kind=kCustom, calls=%fused_computation.1 | custom fusion | bytes 4198400 | tf_op jit(solution)/shard_map/jit(_take)/gather | solution.py:221
  44.6 19.1 collective-permute-done.1
  65.3 23.5 %collective-permute-done.4 = f32[256,1024]{1,0:T(8,128)} collective-permute-done((f32[256,1024]{1,0:T(8,128)S(1)}, f32[256,1024]{1,0:T(8,128)}, u32[]{:S(2)}, u32[]{:S(2)}) %collective-permute-start.4) | collective-permute-done | bytes 1048608 | tf_op jit(solution)/shard_map/ppermute | solution.py:197
  94.4 12.3 gather_fusion.3
  113.2 12.5 gather_fusion.5
  138.4 67.2 %collective-permute-done.5 = f32[128,2048]{1,0:T(8,128)} collective-permute-done((f32[128,2048]{1,0:T(8,128)}, f32[128,2048]{1,0:T(8,128)}, u32[]{:S(2)}, u32[]{:S(2)}) %collective-permute-start.5) | collective-permute-done | bytes 1048608 | tf_op jit(solution)/shard_map/ppermute | solution.py:197
  212.6 20.3 %gather_fusion = bf16[1024,1024]{1,0:T(8,128)(2,1)} fusion(bf16[25152,1024]{1,0:T(8,128)(2,1)} %param.16, s32[1024]{0:T(1024)S(1)} %broadcast_clamp_fusion.1), kind=kCustom, calls=%fused_computation | custom fusion | bytes 4198400 | tf_op jit(solution)/shard_map/jit(_take)/gather | solution.py:221
  233.3 12.2 gather_fusion.2
  246.1 12.4 gather_fusion.4
  289.2 11.4 add_convert_fusion.5
  300.6 51.3 %attention.3 = (bf16[4,256,1024]{2,1,0:T(8,128)(2,1)S(1)}, bf16[4,256,3072]{2,1,0:T(8,128)(2,1)S(1)}) custom-call(bf16[4,256,3072]{2,1,0:T(8,128)(2,1)} %bitcast.242, bf16[4,256,1024]{2,1,0:T(8,128)(2,1)S(1)} %bitcast.173, f32[256,128]{1,0:T(8,128)S(1)} %copy.41.cos_ref, f32[256,128]{1,0:T(8,128)S(1)} %copy.42.sin_ref, ...), custom_call_target="tpu_custom_call" | custom-call | flops 25769803776 | bytes 16777216 | tf_op jit(solution)/shard_map/attention/pallas_call | solution.py:97
  367.1 13.3 convolution_convert_fusion.2
  385.1 15.2 add_convert_fusion.4
  400.3 12.3 fusion.26
  412.6 17.2 fusion.60
  429.8 17.5 fusion.62
  456.1 11.9 convolution_convert_fusion.11
  468.1 17.2 fusion.37
  506.3 11.8 fusion.79
  522.8 20.1 %convolution_convert_fusion.1 = bf16[1536,4096]{1,0:T(8,128)(2,1)} fusion(bf16[1536,1024]{1,0:T(8,128)(2,1)} %bitcast.201, bf16[2048,1024]{1,0:T(8,128)(2,1)} %copy-done.31, bf16[2048,1024]{1,0:T(8,128)(2,1)} %param.27), kind=kOutput, calls=%fused_computation.59 | convolution fusion | flops 12907970560 | bytes 24117248 | tf_op jit(solution)/shard_map/dot_general | solution.py:20
  563.0 18.2 add_convert_fusion.3
  581.3 77.1 %attention.4 = (bf16[6,256,1024]{2,1,0:T(8,128)(2,1)S(1)}, bf16[6,256,3072]{2,1,0:T(8,128)(2,1)}) custom-call(bf16[6,256,3072]{2,1,0:T(8,128)(2,1)} %bitcast.241, bf16[6,256,1024]{2,1,0:T(8,128)(2,1)S(1)} %bitcast.168, f32[256,128]{1,0:T(8,128)S(1)} %copy.41.cos_ref, f32[256,128]{1,0:T(8,128)S(1)} %copy.42.sin_ref, ...), custom_call_target="tpu_custom_call" | custom-call | flops 38654705664 | bytes 25165824 | tf_op jit(solution)/shard_map/attention/pallas_call | solution.py:97
  664.4 20.2 %add_convert_fusion.1 = bf16[1536,4096]{1,0:T(8,128)(2,1)} fusion(bf16[1536,1024]{1,0:T(8,128)(2,1)S(1)} %add_convert_fusion.14, f32[4096]{0:T(1024)S(1)} %copy-done.80, bf16[1024,2048]{1,0:T(8,128)(2,1)} %copy-done.30, bf16[1024,2048]{1,0:T(8,128)(2,1)} %param.25), kind=kOutput, calls=%fused_computation.42 | convolution fusion | flops 12914262016 | bytes 24133632 | tf_op jit(solution)/shard_map/dot_general | solution.py:20
  684.6 24.8 %fusion.8 = (bf16[1536,4096]{1,0:T(8,128)(2,1)}, f32[1536,4096]{1,0:T(8,128)}) fusion(bf16[1536,4096]{1,0:T(8,128)(2,1)} %add_convert_fusion.1, bf16[1536,4096]{1,0:T(8,128)(2,1)} %convolution_convert_fusion.1), kind=kLoop, calls=%fused_computation.29 | loop fusion | flops 75497472 | bytes 62914560 | tf_op jit(solution)/shard_map/convert_element_type | solution.py:289
  709.4 22.8 %fusion.68 = f32[1536,1024]{1,0:T(8,128)} fusion(f32[1536,4096]{1,0:T(8,128)} %get-tuple-element.137, bf16[1536,4096]{1,0:T(8,128)(2,1)} %add_convert_fusion.1, bf16[2048,1024]{1,0:T(8,128)(2,1)} %copy-done.31, bf16[2048,1024]{1,0:T(8,128)(2,1)} %param.27), kind=kOutput, calls=%fused_computation.290 | convolution fusion | flops 12920553472 | bytes 52428800 | tf_op jit(solution)/shard_map/dot_general | solution.py:20
  741.9 29.4 %convolution_add_fusion.1 = f32[4096,1024]{1,0:T(8,128)} fusion(f32[4096,1024]{1,0:T(8,128)} %fusion.60, bf16[1536,1024]{1,0:T(8,128)(2,1)} %bitcast.202, f32[1536,4096]{1,0:T(8,128)} %get-tuple-element.137, bf16[1536,4096]{1,0:T(8,128)(2,1)} %add_convert_fusion.1), kind=kOutput, calls=%fused_computation.75 | convolution fusion | flops 12907970560 | bytes 74448896 | tf_op jit(solution)/shard_map/dot_general | solution.py:20
  771.3 15.4 convolution_convert_fusion.6
  786.8 25.4 %fusion.31 = (f32[1024]{0:T(1024)S(1)}, f32[1536]{0:T(1024)S(1)}, f32[1024]{0:T(1024)S(1)}, f32[1536]{0:T(1024)S(1)}, f32[1024]{0:T(1024)S(1)}, /*index=5*/f32[1024]{0:T(1024)S(1)}, bf16[1536,1024]{1,0:T(8,128)(2,1)}) fusion(f32[1536,1024]{1,0:T(8,128)} %copy-done.6, f32[1024]{0:T(1024)S(1)} %copy-done.48, f32[1024]{0:T(1024)S(1)} %copy-done.52, ...), kind=kOutput, calls=%fused_computation.91 | convolution fusion | flops 12925265920 | bytes 33591296 | tf_op jit(solution)/shard_map/dot_general | solution.py:20
  823.0 15.3 convolution_add_fusion.5
  841.3 22.2 %convolution_add_fusion.3 = f32[1024,4096]{1,0:T(8,128)} fusion(f32[1024,4096]{1,0:T(8,128)} %fusion.79, bf16[1536,1024]{1,0:T(8,128)(2,1)S(1)} %copy-done.20, bf16[1536,4096]{1,0:T(8,128)(2,1)} %get-tuple-element.79), kind=kOutput, calls=%fused_computation.77 | convolution fusion | flops 12889096192 | bytes 49283072 | tf_op jit(solution)/shard_map/dot_general | solution.py:20
  869.5 20.0 %convolution_convert_fusion = bf16[1536,4096]{1,0:T(8,128)(2,1)} fusion(bf16[1536,1024]{1,0:T(8,128)(2,1)} %bitcast.197, bf16[2048,1024]{1,0:T(8,128)(2,1)} %copy-done.31, bf16[2048,1024]{1,0:T(8,128)(2,1)} %param.27), kind=kOutput, calls=%fused_computation.58 | convolution fusion | flops 12907970560 | bytes 24117248 | tf_op jit(solution)/shard_map/dot_general | solution.py:20
  908.5 18.3 add_convert_fusion.2
  927.9 20.2 %add_convert_fusion = bf16[1536,4096]{1,0:T(8,128)(2,1)} fusion(bf16[1536,1024]{1,0:T(8,128)(2,1)S(1)} %add_convert_fusion.10, f32[4096]{0:T(1024)S(1)} %copy-done.81, bf16[1024,2048]{1,0:T(8,128)(2,1)} %copy-done.30, bf16[1024,2048]{1,0:T(8,128)(2,1)} %param.25), kind=kOutput, calls=%fused_computation.41 | convolution fusion | flops 12914262016 | bytes 24133632 | tf_op jit(solution)/shard_map/dot_general | solution.py:20
  948.1 24.6 %fusion.17 = (bf16[1536,4096]{1,0:T(8,128)(2,1)}, f32[1536,4096]{1,0:T(8,128)}) fusion(bf16[1536,4096]{1,0:T(8,128)(2,1)} %add_convert_fusion, bf16[1536,4096]{1,0:T(8,128)(2,1)} %convolution_convert_fusion), kind=kLoop, calls=%fused_computation.38 | loop fusion | flops 75497472 | bytes 62914560 | tf_op jit(solution)/shard_map/convert_element_type | solution.py:289
  972.7 23.1 %fusion.65 = f32[1536,1024]{1,0:T(8,128)} fusion(f32[1536,4096]{1,0:T(8,128)} %get-tuple-element.133, bf16[1536,4096]{1,0:T(8,128)(2,1)} %add_convert_fusion, bf16[2048,1024]{1,0:T(8,128)(2,1)} %copy-done.31, bf16[2048,1024]{1,0:T(8,128)(2,1)} %param.27), kind=kOutput, calls=%fused_computation.289 | convolution fusion | flops 12920553472 | bytes 52428800 | tf_op jit(solution)/shard_map/dot_general | solution.py:20
  995.8 77.0 %attention.5 = (bf16[6,256,1024]{2,1,0:T(8,128)(2,1)S(1)}, bf16[6,256,3072]{2,1,0:T(8,128)(2,1)}) custom-call(bf16[6,256,3072]{2,1,0:T(8,128)(2,1)} %bitcast.240, bf16[6,256,1024]{2,1,0:T(8,128)(2,1)S(1)} %bitcast.167, f32[256,128]{1,0:T(8,128)S(1)} %copy.41.cos_ref, f32[256,128]{1,0:T(8,128)S(1)} %copy.42.sin_ref, ...), custom_call_target="tpu_custom_call" | custom-call | flops 38654705664 | bytes 25165824 | tf_op jit(solution)/shard_map/attention/pallas_call | solution.py:97
  1086.9 28.6 %convolution_add_fusion = f32[4096,1024]{1,0:T(8,128)} fusion(f32[4096,1024]{1,0:T(8,128)} %convolution_add_fusion.1, bf16[1536,1024]{1,0:T(8,128)(2,1)S(1)} %bitcast.199, f32[1536,4096]{1,0:T(8,128)} %get-tuple-element.133, bf16[1536,4096]{1,0:T(8,128)(2,1)} %add_convert_fusion), kind=kOutput, calls=%fused_computation.74 | convolution fusion | flops 12907970560 | bytes 74448896 | tf_op jit(solution)/shard_map/dot_general | solution.py:20
  1115.5 50.4 %collective-permute-done.11 = f32[8,1024,128]{2,1,0:T(8,128)} collective-permute-done((f32[8,1024,128]{2,1,0:T(8,128)}, f32[8,1024,128]{2,1,0:T(8,128)}, u32[]{:S(2)}, u32[]{:S(2)}) %collective-permute-start.11) | collective-permute-done | bytes 4194336 | tf_op jit(solution)/shard_map/ppermute | solution.py:197
  1166.0 15.4 convolution_convert_fusion.4
  1181.4 25.0 %fusion.34 = (f32[1024]{0:T(1024)S(1)}, f32[1536]{0:T(1024)S(1)}, f32[1024]{0:T(1024)S(1)}, f32[1536]{0:T(1024)S(1)}, f32[1024]{0:T(1024)S(1)}, /*index=5*/f32[1024]{0:T(1024)S(1)}, bf16[1536,1024]{1,0:T(8,128)(2,1)}) fusion(f32[1536,1024]{1,0:T(8,128)} %copy-done.5, f32[1024]{0:T(1024)S(1)} %copy-done.49, f32[1024]{0:T(1024)S(1)} %copy-done.53, ...), kind=kOutput, calls=%fused_computation.94 | convolution fusion | flops 12925265920 | bytes 33591296 | tf_op jit(solution)/shard_map/dot_general | solution.py:20
  1218.4 16.1 convolution_add_fusion.4
  1236.4 25.4 %convolution_add_fusion.2 = f32[1024,4096]{1,0:T(8,128)} fusion(f32[1024,4096]{1,0:T(8,128)} %convolution_add_fusion.3, bf16[1536,1024]{1,0:T(8,128)(2,1)S(1)} %copy-done.18, bf16[1536,4096]{1,0:T(8,128)(2,1)} %get-tuple-element.91), kind=kOutput, calls=%fused_computation.76 | convolution fusion | flops 12889096192 | bytes 49283072 | tf_op jit(solution)/shard_map/dot_general | solution.py:20
  1262.6 11.3 all-gather
  1321.9 386.0 %psum.7 = f32[12288]{0:T(1024)S(1)} all-reduce(f32[12288]{0:T(1024)S(1)} %constant_dynamic-update-slice_fusion.20), channel_id=1, replica_groups=mesh['tp'=2,'dp'=8] {'tp','dp'}, use_global_device_ids=true, to_apply=%region_33.34 | all-reduce | flops 12288 | bytes 98304 | tf_op jit(solution)/shard_map/psum | solution.py:347
  1713.8 10.1 add_convert_fusion.8
  1731.8 101.8 %scatter_rows.2.refs_4_ = f32[25152,128]{1,0:T(8,128)} custom-call(s32[4,1,2048]{2,1,0:T(1,128)S(1)} %reshape_reshape.20.refs_0_, s32[4,1,2048]{2,1,0:T(1,128)S(1)} %reshape_reshape.21.refs_1_, s32[6,1,2048]{2,1,0:T(1,128)S(1)} %reshape_reshape.26.refs_2_, s32[6,1,2048]{2,1,0:T(1,128)S(1)} %reshape_reshape.27.refs_3_, f32[8192,128]{1,0:T(8,128)} %bitcast.39.refs_4_, ...), custom_call_target="tpu_custom_call" | custom-call | flops 122880000000 | bytes 41943040 | tf_op jit(solution)/shard_map/scatter_rows/pallas_call | solution.py:178
  1844.1 26.4 %collective-permute-done.12 = f32[8,1536,128]{2,1,0:T(8,128)} collective-permute-done((f32[8,1536,128]{2,1,0:T(8,128)}, f32[8,1536,128]{2,1,0:T(8,128)}, u32[]{:S(2)}, u32[]{:S(2)}) %collective-permute-start.12) | collective-permute-done | bytes 6291488 | tf_op jit(solution)/shard_map/ppermute | solution.py:197
  1870.5 72.9 %scatter_rows.3 = f32[25152,128]{1,0:T(8,128)} custom-call(s32[6,1,2048]{2,1,0:T(1,128)S(1)} %reshape_reshape.24.refs_0_, s32[6,1,2048]{2,1,0:T(1,128)S(1)} %reshape_reshape.25.refs_1_, f32[12288,128]{1,0:T(8,128)} %bitcast.37.refs_2_, f32[12288,128]{1,0:T(8,128)} %bitcast.38.refs_3_, f32[25152,128]{1,0:T(8,128)} %scatter_rows.2.refs_4_), custom_call_target="tpu_custom_call" | custom-call | flops 73728000000 | bytes 25165824 | tf_op jit(solution)/shard_map/scatter_rows/pallas_call | solution.py:178
  (471 shorter events, 318.1 us)
Async XLA Ops:
  7.2 252.7 %all-gather.8.cloned.1.call-start = ((), (), s32[]{:S(2)}) async-start(), calls=%async_computation.8 | async-start | bytes 2359296 | tf_op jit(solution)/shard_map/all_gather | solution.py:214
  8.2 29.1 %collective-permute-start.3 = (f32[64,1024]{1,0:T(8,128)S(1)}, f32[64,1024]{1,0:T(8,128)}, u32[]{:S(2)}, u32[]{:S(2)}) collective-permute-start(f32[64,1024]{1,0:T(8,128)S(1)} %dynamic-slice_convert_fusion.3), channel_id=1, source_target_pairs={{0,8},{8,0},{1,9},{9,1},{2,10},{10,2},{3,11},{11,3},{4,12},{12,4},... | collective-permute-start | bytes 786440 | tf_op jit(solution)/shard_map/ppermute | solution.py:197
  37.3 243.0 %all-gather.6.cloned.1.call-start = ((), (), s32[]{:S(2)}) async-start(), calls=%async_computation.7 | async-start | bytes 7077888 | tf_op jit(solution)/shard_map/all_gather | solution.py:214
  40.1 53.5 %copy-start.82 = (bf16[8,3,64]{2,0,1:T(8,128)(2,1)S(1)}, bf16[8,3,64]{2,0,1:T(8,128)(2,1)}, u32[]{:S(2)}) copy-start(bf16[8,3,64]{2,0,1:T(8,128)(2,1)} %param.22) | copy-start | bytes 9220
  40.1 53.6 %copy-start.87 = (bf16[2048]{0:T(1024)(128)(2,1)S(1)}, bf16[2048]{0:T(1024)(128)(2,1)}, u32[]{:S(2)}) copy-start(bf16[2048]{0:T(1024)(128)(2,1)} %param.26) | copy-start | bytes 12292
  40.1 54.2 %copy-start.44 = (s32[32,256]{1,0:T(8,128)S(1)}, s32[32,256]{1,0:T(8,128)}, u32[]{:S(2)}) copy-start(s32[32,256]{1,0:T(8,128)} %param.15) | copy-start | bytes 98308
  44.5 19.1 collective-permute-start.1
  63.7 296.6 %all-gather.10.cloned.1.call-start = ((), (), s32[]{:S(2)}) async-start(), calls=%async_computation.9 | async-start | bytes 9437184 | tf_op jit(solution)/shard_map/all_gather | solution.py:214
  64.9 23.9 %collective-permute-start.4 = (f32[256,1024]{1,0:T(8,128)S(1)}, f32[256,1024]{1,0:T(8,128)}, u32[]{:S(2)}, u32[]{:S(2)}) collective-permute-start(f32[256,1024]{1,0:T(8,128)S(1)} %dynamic-slice_convert_fusion.1), channel_id=1, source_target_pairs={{0,8},{8,0},{1,9},{9,1},{2,10},{10,2},{3,11},{11,3},{4,12},{12,4},... | collective-permute-start | bytes 3145736 | tf_op jit(solution)/shard_map/ppermute | solution.py:197
  88.8 291.5 %all-gather.12.cloned.1.call-start = ((), (), s32[]{:S(2)}) async-start(), calls=%async_computation.10 | async-start | bytes 9437184 | tf_op jit(solution)/shard_map/all_gather | solution.py:214
  89.4 177.0 %collective-permute-start = (f32[1024,1024]{1,0:T(8,128)}, f32[1024,1024]{1,0:T(8,128)}, u32[]{:S(2)}, u32[]{:S(2)}) collective-permute-start(f32[1024,1024]{1,0:T(8,128)} %select_convert_fusion.2), channel_id=1, source_target_pairs={{0,8},{8,0},{1,9},{9,1},{2,10},{10,2},{3,11},{11,3},{4,12},{12,4},... | collective-permute-start | bytes 12582920 | tf_op jit(solution)/shard_map/ppermute | solution.py:197
  92.1 113.5 %collective-permute-start.5 = (f32[128,2048]{1,0:T(8,128)}, f32[128,2048]{1,0:T(8,128)}, u32[]{:S(2)}, u32[]{:S(2)}) collective-permute-start(f32[128,2048]{1,0:T(8,128)} %dynamic-slice_convert_fusion), channel_id=1, source_target_pairs={{0,8},{8,0},{1,9},{9,1},{2,10},{10,2},{3,11},{11,3},{4,12},{12,4},... | collective-permute-start | bytes 3145736 | tf_op jit(solution)/shard_map/ppermute | solution.py:197
  93.6 166.1 %collective-permute-start.2 = (f32[3584]{0:T(1024)S(1)}, f32[3584]{0:T(1024)S(1)}, u32[]{:S(2)}, u32[]{:S(2)}) collective-permute-start(f32[3584]{0:T(1024)S(1)} %maximum_convert_fusion), channel_id=1, source_target_pairs={{0,8},{8,0},{1,9},{9,1},{2,10},{10,2},{3,11},{11,3},{4,12},{12,4},... | collective-permute-start | bytes 43016 | tf_op jit(solution)/shard_map/ppermute | solution.py:197
  111.7 406.3 %collective-permute-start.7 = (f32[1536,1024]{1,0:T(8,128)}, f32[1536,1024]{1,0:T(8,128)}, u32[]{:S(2)}, u32[]{:S(2)}) collective-permute-start(f32[1536,1024]{1,0:T(8,128)} %select_convert_fusion.1), channel_id=1, source_target_pairs={{0,8},{8,0},{1,9},{9,1},{2,10},{10,2},{3,11},{11,3},{4,12},{12,4},... | collective-permute-start | bytes 18874376 | tf_op jit(solution)/shard_map/ppermute | solution.py:197
  130.7 732.9 %collective-permute-start.9 = (f32[1536,1024]{1,0:T(8,128)}, f32[1536,1024]{1,0:T(8,128)}, u32[]{:S(2)}, u32[]{:S(2)}) collective-permute-start(f32[1536,1024]{1,0:T(8,128)} %select_convert_fusion), channel_id=1, source_target_pairs={{0,8},{8,0},{1,9},{9,1},{2,10},{10,2},{3,11},{11,3},{4,12},{12,4},... | collective-permute-start | bytes 18874376 | tf_op jit(solution)/shard_map/ppermute | solution.py:197
  233.0 39.4 %copy-start.50 = (f32[1024]{0:T(1024)}, f32[1024]{0:T(1024)S(1)}, u32[]{:S(2)}) copy-start(f32[1024]{0:T(1024)S(1)} %convert_element_type.249) | copy-start | bytes 12292
  233.0 39.3 %copy-start.62 = (f32[1024]{0:T(1024)}, f32[1024]{0:T(1024)S(1)}, u32[]{:S(2)}) copy-start(f32[1024]{0:T(1024)S(1)} %convert_element_type.250) | copy-start | bytes 12292
  233.0 43.3 %copy-start.46 = (f32[1024]{0:T(1024)}, f32[1024]{0:T(1024)S(1)}, u32[]{:S(2)}) copy-start(f32[1024]{0:T(1024)S(1)} %convert_element_type.263) | copy-start | bytes 12292
  233.0 43.3 %copy-start.58 = (f32[1024]{0:T(1024)}, f32[1024]{0:T(1024)S(1)}, u32[]{:S(2)}) copy-start(f32[1024]{0:T(1024)S(1)} %convert_element_type.264) | copy-start | bytes 12292
  259.7 125.3 %copy-start.79 = (f32[4096]{0:T(1024)}, f32[4096]{0:T(1024)S(1)}, u32[]{:S(2)}) copy-start(f32[4096]{0:T(1024)S(1)} %pad_maximum_fusion.4) | copy-start | bytes 49156
  259.8 29.4 %copy-start.95 = (f32[3072]{0:T(1024)}, f32[3072]{0:T(1024)S(1)}, u32[]{:S(2)}) copy-start(f32[3072]{0:T(1024)S(1)} %constant_dynamic-update-slice_fusion.18) | copy-start | bytes 36868
  300.6 55.3 %copy-start.26 = (bf16[4,256,1024]{2,1,0:T(8,128)(2,1)S(1)}, bf16[4,256,1024]{2,1,0:T(8,128)(2,1)}, u32[]{:S(2)}) copy-start(bf16[4,256,1024]{2,1,0:T(8,128)(2,1)} %get-tuple-element.141) | copy-start | bytes 6291460
  456.1 33.8 %slice-start = ((s8[6291456]{0:T(1024)(128)(4,1)}), s8[4194304]{0:T(1024)(128)(4,1)S(1)}, s32[]{:S(2)}) async-start(s8[6291456]{0:T(1024)(128)(4,1)} %bitcast.163), calls=%async_computation.15 | async-start | bytes 8388608
  542.9 228.4 %all-to-all-start = ((f32[8,1024,128]{2,1,0:T(8,128)}), f32[8,1024,128]{2,1,0:T(8,128)}, u32[]{:S(2)}, u32[]{:S(2)}) async-start(f32[8,1024,128]{2,1,0:T(8,128)} %bitcast_bitcast_fusion.2), calls=%async_computation | async-start | bytes 8388608 | tf_op jit(solution)/shard_map/all_to_all | solution.py:302
  548.0 567.5 %collective-permute-start.6 = (f32[1024,1024]{1,0:T(8,128)}, f32[1024,1024]{1,0:T(8,128)}, u32[]{:S(2)}, u32[]{:S(2)}) collective-permute-start(f32[1024,1024]{1,0:T(8,128)} %add_add_fusion.2), channel_id=1, source_target_pairs={{0,8},{8,0},{1,9},{9,1},{2,10},{10,2},{3,11},{11,3},{4,12},{12,4},... | collective-permute-start | bytes 12582920 | tf_op jit(solution)/shard_map/ppermute | solution.py:197
  563.0 100.4 %copy-start.6 = (f32[1536,1024]{1,0:T(8,128)}, f32[1536,1024]{1,0:T(8,128)S(1)}, u32[]{:S(2)}) copy-start(f32[1536,1024]{1,0:T(8,128)S(1)} %get-tuple-element.139) | copy-start | bytes 18874372
  581.3 77.1 %copy-start.24 = (bf16[6,256,1024]{2,1,0:T(8,128)(2,1)S(1)}, bf16[6,256,1024]{2,1,0:T(8,128)(2,1)}, u32[]{:S(2)}) copy-start(bf16[6,256,1024]{2,1,0:T(8,128)(2,1)} %get-tuple-element.147) | copy-start | bytes 9437188
  581.3 77.1 %copy-start.99 = (f32[1024,1024]{1,0:T(8,128)S(1)}, f32[1024,1024]{1,0:T(8,128)}, u32[]{:S(2)}) copy-start(f32[1024,1024]{1,0:T(8,128)} %convolution_bitcast_fusion) | copy-start | bytes 12582916
  889.5 276.4 %all-to-all-start.1 = ((f32[8,1536,128]{2,1,0:T(8,128)}), f32[8,1536,128]{2,1,0:T(8,128)}, u32[]{:S(2)}, u32[]{:S(2)}) async-start(f32[8,1536,128]{2,1,0:T(8,128)} %bitcast.188), calls=%async_computation.1 | async-start | bytes 12582912 | tf_op jit(solution)/shard_map/all_to_all | solution.py:302
  894.4 815.4 %reduce-scatter.9.cloned.1.call-start = ((), (), s32[]{:S(2)}) async-start(), calls=%async_computation.13 | async-start | bytes 4718592 | tf_op jit(solution)/shard_map/reduce_scatter | solution.py:331
  995.8 78.0 %copy-start.8 = (bf16[1536,1024]{1,0:T(8,128)(2,1)S(1)}, bf16[1536,1024]{1,0:T(8,128)(2,1)}, u32[]{:S(2)}) copy-start(bf16[1536,1024]{1,0:T(8,128)(2,1)} %gather_fusion.4) | copy-start | bytes 9437188
  995.8 78.0 %copy-start.42 = (bf16[512,1024]{1,0:T(8,128)(2,1)S(1)}, bf16[512,1024]{1,0:T(8,128)(2,1)}, u32[]{:S(2)}) copy-start(bf16[512,1024]{1,0:T(8,128)(2,1)} %copy-done.39) | copy-start | bytes 3145732
  995.8 78.0 %copy-start.78 = (bf16[8,64,1024]{2,1,0:T(8,128)(2,1)S(1)}, bf16[8,64,1024]{2,1,0:T(8,128)(2,1)}, u32[]{:S(2)}) copy-start(bf16[8,64,1024]{2,1,0:T(8,128)(2,1)} %param.23) | copy-start | bytes 3145732
  995.8 78.0 %copy-start.98 = (f32[1536,1024]{1,0:T(8,128)S(1)}, f32[1536,1024]{1,0:T(8,128)}, u32[]{:S(2)}) copy-start(f32[1536,1024]{1,0:T(8,128)} %fusion.65) | copy-start | bytes 18874372
  1072.8 93.1 %collective-permute-start.11 = (f32[8,1024,128]{2,1,0:T(8,128)}, f32[8,1024,128]{2,1,0:T(8,128)}, u32[]{:S(2)}, u32[]{:S(2)}) collective-permute-start(f32[8,1024,128]{2,1,0:T(8,128)} %all-to-all-done), channel_id=1, source_target_pairs={{0,8},{8,0},{1,9},{9,1},{2,10},{10,2},{3,11},{11,3},{4,12},{12,4},... | collective-permute-start | bytes 12582920 | tf_op jit(solution)/shard_map/ppermute | solution.py:197
  1086.9 746.7 %reduce-scatter.5.cloned.1.call-start = ((), (), s32[]{:S(2)}) async-start(), calls=%async_computation.11 | async-start | bytes 14155776 | tf_op jit(solution)/shard_map/reduce_scatter | solution.py:331
  1234.6 603.9 %reduce-scatter.7.cloned.1.call-start = ((), (), s32[]{:S(2)}) async-start(), calls=%async_computation.12 | async-start | bytes 18874368 | tf_op jit(solution)/shard_map/reduce_scatter | solution.py:331
  1235.3 605.4 %reduce-scatter.11.cloned.1.call-start = ((), (), s32[]{:S(2)}) async-start(), calls=%async_computation.14 | async-start | bytes 18874368 | tf_op jit(solution)/shard_map/reduce_scatter | solution.py:331
  1274.5 439.3 %collective-permute-start.8 = (f32[1536,1024]{1,0:T(8,128)}, f32[1536,1024]{1,0:T(8,128)}, u32[]{:S(2)}, u32[]{:S(2)}) collective-permute-start(f32[1536,1024]{1,0:T(8,128)} %add_add_fusion.1), channel_id=1, source_target_pairs={{0,8},{8,0},{1,9},{9,1},{2,10},{10,2},{3,11},{11,3},{4,12},{12,4},... | collective-permute-start | bytes 18874376 | tf_op jit(solution)/shard_map/ppermute | solution.py:197
  1274.8 439.0 %collective-permute-start.10 = (f32[1536,1024]{1,0:T(8,128)}, f32[1536,1024]{1,0:T(8,128)}, u32[]{:S(2)}, u32[]{:S(2)}) collective-permute-start(f32[1536,1024]{1,0:T(8,128)} %add_add_fusion), channel_id=1, source_target_pairs={{0,8},{8,0},{1,9},{9,1},{2,10},{10,2},{3,11},{11,3},{4,12},{12,4},... | collective-permute-start | bytes 18874376 | tf_op jit(solution)/shard_map/ppermute | solution.py:197
  1302.4 429.3 %all-to-all-start.2 = ((f32[8,1536,128]{2,1,0:T(8,128)}), f32[8,1536,128]{2,1,0:T(8,128)}, u32[]{:S(2)}, u32[]{:S(2)}) async-start(f32[8,1536,128]{2,1,0:T(8,128)} %bitcast.187), calls=%async_computation.2 | async-start | bytes 12582912 | tf_op jit(solution)/shard_map/all_to_all | solution.py:302
  1307.4 424.4 %collective-permute-start.13 = (f32[8,1536,128]{2,1,0:T(8,128)}, f32[8,1536,128]{2,1,0:T(8,128)}, u32[]{:S(2)}, u32[]{:S(2)}) collective-permute-start(f32[8,1536,128]{2,1,0:T(8,128)} %all-to-all-done.1), channel_id=1, source_target_pairs={{0,8},{8,0},{1,9},{9,1},{2,10},{10,2},{3,11},{11,3},{4,12},{12,4},... | collective-permute-start | bytes 18874376 | tf_op jit(solution)/shard_map/ppermute | solution.py:197
  1711.5 231.8 %collective-permute-start.15 = (f32[512,128]{1,0:T(8,128)}, f32[512,128]{1,0:T(8,128)}, u32[]{:S(2)}, u32[]{:S(2)}) collective-permute-start(f32[512,128]{1,0:T(8,128)} %slice.204), channel_id=1, source_target_pairs={{0,8},{8,0},{1,9},{9,1},{2,10},{10,2},{3,11},{11,3},{4,12},{12,4},... | collective-permute-start | bytes 786440 | tf_op jit(solution)/shard_map/ppermute | solution.py:197
  1731.8 138.7 %collective-permute-start.12 = (f32[8,1536,128]{2,1,0:T(8,128)}, f32[8,1536,128]{2,1,0:T(8,128)}, u32[]{:S(2)}, u32[]{:S(2)}) collective-permute-start(f32[8,1536,128]{2,1,0:T(8,128)} %all-to-all-done.2), channel_id=1, source_target_pairs={{0,8},{8,0},{1,9},{9,1},{2,10},{10,2},{3,11},{11,3},{4,12},{12,4},... | collective-permute-start | bytes 18874376 | tf_op jit(solution)/shard_map/ppermute | solution.py:197
  1836.4 107.0 %collective-permute-start.17 = (f32[128,1536]{0,1:T(8,128)}, f32[128,1536]{0,1:T(8,128)}, u32[]{:S(2)}, u32[]{:S(2)}) collective-permute-start(f32[128,1536]{0,1:T(8,128)} %bitcast.46), channel_id=1, source_target_pairs={{0,8},{8,0},{1,9},{9,1},{2,10},{10,2},{3,11},{11,3},{4,12},{12,4},... | collective-permute-start | bytes 2359304 | tf_op jit(solution)/shard_map/ppermute | solution.py:197
  1840.7 102.7 %collective-permute-start.14 = (f32[2048,128]{1,0:T(8,128)}, f32[2048,128]{1,0:T(8,128)S(1)}, u32[]{:S(2)}, u32[]{:S(2)}) collective-permute-start(f32[2048,128]{1,0:T(8,128)} %slice.203), channel_id=1, source_target_pairs={{0,8},{8,0},{1,9},{9,1},{2,10},{10,2},{3,11},{11,3},{4,12},{12,4},... | collective-permute-start | bytes 3145736 | tf_op jit(solution)/shard_map/ppermute | solution.py:197
  1842.0 101.4 %collective-permute-start.16 = (f32[128,2048]{1,0:T(8,128)S(1)}, f32[128,2048]{1,0:T(8,128)S(1)}, u32[]{:S(2)}, u32[]{:S(2)}) collective-permute-start(f32[128,2048]{1,0:T(8,128)S(1)} %slice.205), channel_id=1, source_target_pairs={{0,8},{8,0},{1,9},{9,1},{2,10},{10,2},{3,11},{11,3},{4,12},{12,4},... | collective-permute-start | bytes 3145736 | tf_op jit(solution)/shard_map/ppermute | solution.py:197
  1870.5 75.3 %copy-start.36 = (f32[4096,128]{1,0:T(8,128)S(1)}, f32[4096,128]{1,0:T(8,128)}, u32[]{:S(2)}) copy-start(f32[4096,128]{1,0:T(8,128)} %reduce-scatter.7.cloned.1.call-done) | copy-start | bytes 6291460
  (94 other events, 1013.5 us)
Sparse Core Ops, SparseCore 0:
  37.4 24.0 all-gather.7
  63.8 41.5 all-gather.5
  107.3 50.4 all-gather.9
  205.8 50.5 all-gather.11
  1087.0 46.3 reduce-scatter.8
  1234.7 99.1 reduce-scatter.4
  1337.4 128.2 reduce-scatter.6
  1469.3 110.5 reduce-scatter.10

commit v3 on v2

--- a/solution.py
+++ b/solution.py
@@ -207,18 +207,21 @@
         own_at, peer_at = tp_i * half_seq, (1 - tp_i) * half_seq
         zero = jnp.where(token_ids[0, 0] < 0, 1.0, 0.0).astype(F32)
 
-        def from_peer(w):
+        def from_peer(w, ready):
             size = w.shape[0] // n_dp
             piece = swap(lax.dynamic_slice_in_dim(w, dp_i * size, size, 0).astype(F32))
-            piece, _ = lax.optimization_barrier((piece, first_rows))
+            piece, _ = lax.optimization_barrier((piece, ready))
             whole = lax.all_gather(piece, 'dp', axis=0, tiled=True)
             return (whole + zero).astype(BF16)
 
-        def rows_of(ids):
+        def pick_rows(ids):
             local = ids - tp_i * vocab_local
             ok = (local >= 0) & (local < vocab_local)
             other = jnp.where(local < 0, local + vocab_local, local - vocab_local)
             picked = jnp.take(embed_table, jnp.where(ok, local, other), axis=0, mode='clip')
+            return picked, ok
+
+        def rows_of(picked, ok):
             return jnp.where(ok[..., None], picked, jnp.zeros_like(picked)).astype(F32)
 
         ids_own = lax.dynamic_slice_in_dim(token_ids, own_at, half_seq, 0)
@@ -228,16 +231,17 @@
         for size in CHUNKS:
             bounds.append((start, start + size))
             start += size
-        first_rows = rows_of(ids_peer[bounds[0][0]:bounds[0][1]].reshape(-1))
-        sent_x = [swap(first_rows)] + [swap(rows_of(ids_peer[a:b].reshape(-1))) for a, b in bounds[1:]]
+        first_rows = rows_of(*pick_rows(ids_peer[bounds[0][0]:bounds[0][1]].reshape(-1)))
+        sent_x = [swap(first_rows)] + [swap(rows_of(*pick_rows(ids_peer[a:b].reshape(-1)))) for a, b in bounds[1:]]
+        picked_own = [pick_rows(ids_own[a:b].reshape(-1)) for a, b in bounds]
 
         wqkv_own = w_qkv.transpose(2, 0, 1, 3).reshape(3 * d_model, attn_local)
-        wqkv_peer = from_peer(wqkv_own)
+        wqkv_peer = from_peer(wqkv_own, first_rows)
         qkv_all = jnp.concatenate([w[i * d_model:(i + 1) * d_model] for i in range(3) for w in (wqkv_own, wqkv_peer)], axis=1)
         dense_own = w_dense.reshape(attn_local, d_model)
-        dense_all = jnp.concatenate([dense_own, from_peer(dense_own)], axis=0)
-        fc1_all = jnp.concatenate([w_fc1, from_peer(w_fc1)], axis=1)
-        fc2_all = jnp.concatenate([w_fc2, from_peer(w_fc2)], axis=0)
+        dense_all = jnp.concatenate([dense_own, from_peer(dense_own, first_rows)], axis=0)
+        fc1_all = jnp.concatenate([w_fc1, from_peer(w_fc1, [p for p, _ in picked_own])], axis=1)
+        fc2_all = jnp.concatenate([w_fc2, from_peer(w_fc2, first_rows)], axis=0)
         bqkv_own = b_qkv.transpose(1, 0, 2).reshape(-1)
         bias_own = jnp.concatenate([bqkv_own, b_fc1]).astype(F32)
         bias_peer = swap(bias_own)
@@ -262,7 +266,7 @@
         t0 = ((0,), (0,))
         total = lambda v: jnp.sum(v.astype(F32), axis=0)
         after, held, older = [], [], []
-        for (a, b), recv_x in zip(bounds, sent_x):
+        for c, ((a, b), recv_x) in enumerate(zip(bounds, sent_x)):
             last = b == half_seq
             tokens = (b - a) * seq_len
             flat = lambda v: v.reshape(tokens, v.shape[-1])
@@ -270,9 +274,11 @@
             cot = flat(cot_own[a:b])
             if after:
                 cot, recv_x, _ = lax.optimization_barrier((cot, recv_x, after))
+            if c == 0:
+                recv_x, local_own, local_peer = lax.optimization_barrier((recv_x, local_own, local_peer))
             grad_act = dot_f32(cot, fc2_all, ((1,), (1,))).astype(BF16)
             grad_ctx = dot_f32(cot, dense_all, ((1,), (1,))).astype(BF16)
-            x = rows_of(ids_own[a:b].reshape(-1)) + recv_x
+            x = rows_of(*picked_own[c]) + recv_x
             centered = x - jnp.mean(x, axis=-1, keepdims=True)
             inv_std = lax.rsqrt(jnp.mean(centered * centered, axis=-1, keepdims=True) + EPS_NORM)
             normed = centered * inv_std

time: 1970 us -> 1910 us (0.970)
  waiting for transfers between devices: 188 us -> 132 us
    ppermute x18, waiting for transfers between devices: 187 us -> 131 us  [swap(): return lax.ppermute(val, 'tp', [(0, 1), (1, 0)])]
  transfers between devices with their start and end apart: 29 -> 29, of which waited for: 5 -> 5; matrix products, arithmetic and copies ran while one was open for 47% -> 49% of each run, Pallas kernels for 19% -> 20%
where the time goes in v3:
time: 1910 us; the launch traced here: 1900 us
  matrix products  563 us (29%)
  blocking collectives  393 us (21%)
  Pallas kernels  380 us (20%)
  other arithmetic  218 us (11%)
  local copies, waits for them, and re-layouts  162 us (8%)
  waiting for transfers between devices  132 us (7%)
  starting transfers between devices  34.4 us (2%)
    dot_general x36, matrix products, dot_f32(): return lax.dot_general(a, b, (dims, ((), ())), preferred_element_type=F32)  563 us
    psum x1, blocking collectives, device_step(): lax.psum(jnp.concatenate(small_sum[:5] + [side[0], side[1]]), ('tp', 'dp'))  382 us
    pallas_call x3, Pallas kernels, attention(): pl.pallas_call(functools.partial(attention_kernel, head_dim), grid=(n,),...  205 us
    pallas_call x2, Pallas kernels, scatter_rows(): pl.pallas_call(functools.partial(scatter_kernel, has_init, rows, block, c...  175 us
    ppermute x18, waiting for transfers between devices, swap(): return lax.ppermute(val, 'tp', [(0, 1), (1, 0)])  131 us
    gather x6, local copies, waits for them, and re-layouts, pick_rows(): jnp.take(embed_table, jnp.where(ok, local, other), axis=0, mode='clip')  89.8 us
    convert_element_type x3, other arithmetic, device_step(): grad_pre = (grad_act.astype(F32) * slope).astype(BF16)  61.3 us
    reduce_sum x9, other arithmetic, device_step(): total = lambda v: jnp.sum(v.astype(F32), axis=0)  50.4 us
  transfers between devices with their start and end apart: 29, of which 5 were waited for; matrix products, arithmetic and copies ran while one was open for 49% of the time, Pallas kernels for 20%

profile of v3, /device:TPU:0, one launch (start us, length us, event | category | flops | bytes accessed | tf_op | source)
XLA Modules:
  0.0 1899.3 jit_solution(2198298307841594896)
XLA Ops:
  13.0 20.1 %gather_fusion.1 = bf16[1024,1024]{1,0:T(8,128)(2,1)} fusion(bf16[25152,1024]{1,0:T(8,128)(2,1)} %param.16, s32[1024]{0:T(1024)S(1)} %broadcast_clamp_fusion), kind=kCustom, calls=%fused_computation.1 | custom fusion | bytes 4198400 | tf_op jit(solution)/shard_map/jit(_take)/gather | solution.py:221
  44.6 19.1 %collective-permute-done.1 = f32[384,512]{0,1:T(8,128)} collective-permute-done((f32[384,512]{0,1:T(8,128)S(1)}, f32[384,512]{0,1:T(8,128)}, u32[]{:S(2)}, u32[]{:S(2)}) %collective-permute-start.1) | collective-permute-done | bytes 786464 | tf_op jit(solution)/shard_map/ppermute | solution.py:197
  65.3 23.5 %collective-permute-done.4 = f32[256,1024]{1,0:T(8,128)} collective-permute-done((f32[256,1024]{1,0:T(8,128)S(1)}, f32[256,1024]{1,0:T(8,128)}, u32[]{:S(2)}, u32[]{:S(2)}) %collective-permute-start.4) | collective-permute-done | bytes 1048608 | tf_op jit(solution)/shard_map/ppermute | solution.py:197
  94.4 12.3 gather_fusion.4
  113.1 12.5 gather_fusion.5
  138.3 10.4 all-gather
  148.8 20.6 %gather_fusion = bf16[1024,1024]{1,0:T(8,128)(2,1)} fusion(bf16[25152,1024]{1,0:T(8,128)(2,1)} %param.16, s32[1024]{0:T(1024)S(1)} %broadcast_clamp_fusion.1), kind=kCustom, calls=%fused_computation | custom fusion | bytes 4198400 | tf_op jit(solution)/shard_map/jit(_take)/gather | solution.py:221
  169.4 12.2 gather_fusion.2
  181.6 12.2 gather_fusion.3
  193.9 11.7 collective-permute-done.5
  245.6 11.6 add_convert_fusion.5
  257.2 51.1 %attention.3 = (bf16[4,256,1024]{2,1,0:T(8,128)(2,1)S(1)}, bf16[4,256,3072]{2,1,0:T(8,128)(2,1)S(1)}) custom-call(bf16[4,256,3072]{2,1,0:T(8,128)(2,1)} %bitcast.243, bf16[4,256,1024]{2,1,0:T(8,128)(2,1)S(1)} %bitcast.173, f32[256,128]{1,0:T(8,128)S(1)} %copy.41.cos_ref, f32[256,128]{1,0:T(8,128)S(1)} %copy.42.sin_ref, ...), custom_call_target="tpu_custom_call" | custom-call | flops 25769803776 | bytes 16777216 | tf_op jit(solution)/shard_map/attention/pallas_call | solution.py:97
  323.5 13.7 convolution_convert_fusion.2
  341.9 15.2 add_convert_fusion.4
  357.1 11.9 fusion.26
  369.0 17.2 fusion.60
  386.2 17.7 fusion.62
  412.7 10.7 convolution_convert_fusion.11
  423.5 17.7 fusion.37
  462.4 12.2 fusion.81
  479.3 20.1 %convolution_convert_fusion.1 = bf16[1536,4096]{1,0:T(8,128)(2,1)} fusion(bf16[1536,1024]{1,0:T(8,128)(2,1)} %bitcast.201, bf16[2048,1024]{1,0:T(8,128)(2,1)} %copy-done.29, bf16[2048,1024]{1,0:T(8,128)(2,1)} %param.27), kind=kOutput, calls=%fused_computation.59 | convolution fusion | flops 12907970560 | bytes 24117248 | tf_op jit(solution)/shard_map/dot_general | solution.py:20
  518.3 18.2 add_convert_fusion.3
  536.5 77.0 %attention.4 = (bf16[6,256,1024]{2,1,0:T(8,128)(2,1)S(1)}, bf16[6,256,3072]{2,1,0:T(8,128)(2,1)}) custom-call(bf16[6,256,3072]{2,1,0:T(8,128)(2,1)} %bitcast.242, bf16[6,256,1024]{2,1,0:T(8,128)(2,1)S(1)} %bitcast.168, f32[256,128]{1,0:T(8,128)S(1)} %copy.41.cos_ref, f32[256,128]{1,0:T(8,128)S(1)} %copy.42.sin_ref, ...), custom_call_target="tpu_custom_call" | custom-call | flops 38654705664 | bytes 25165824 | tf_op jit(solution)/shard_map/attention/pallas_call | solution.py:97
  619.7 20.2 %add_convert_fusion.1 = bf16[1536,4096]{1,0:T(8,128)(2,1)} fusion(bf16[1536,1024]{1,0:T(8,128)(2,1)S(1)} %add_convert_fusion.14, f32[4096]{0:T(1024)S(1)} %copy-done.79, bf16[1024,2048]{1,0:T(8,128)(2,1)} %copy-done.28, bf16[1024,2048]{1,0:T(8,128)(2,1)} %param.25), kind=kOutput, calls=%fused_computation.42 | convolution fusion | flops 12914262016 | bytes 24133632 | tf_op jit(solution)/shard_map/dot_general | solution.py:20
  639.8 24.8 %fusion.8 = (bf16[1536,4096]{1,0:T(8,128)(2,1)}, f32[1536,4096]{1,0:T(8,128)}) fusion(bf16[1536,4096]{1,0:T(8,128)(2,1)} %add_convert_fusion.1, bf16[1536,4096]{1,0:T(8,128)(2,1)} %convolution_convert_fusion.1), kind=kLoop, calls=%fused_computation.29 | loop fusion | flops 75497472 | bytes 62914560 | tf_op jit(solution)/shard_map/convert_element_type | solution.py:295
  664.6 22.8 %fusion.68 = f32[1536,1024]{1,0:T(8,128)} fusion(f32[1536,4096]{1,0:T(8,128)} %get-tuple-element.143, bf16[1536,4096]{1,0:T(8,128)(2,1)} %add_convert_fusion.1, bf16[2048,1024]{1,0:T(8,128)(2,1)} %copy-done.29, bf16[2048,1024]{1,0:T(8,128)(2,1)} %param.27), kind=kOutput, calls=%fused_computation.286 | convolution fusion | flops 12920553472 | bytes 52428800 | tf_op jit(solution)/shard_map/dot_general | solution.py:20
  697.2 29.6 %convolution_add_fusion.1 = f32[4096,1024]{1,0:T(8,128)} fusion(f32[4096,1024]{1,0:T(8,128)} %fusion.60, bf16[1536,1024]{1,0:T(8,128)(2,1)} %bitcast.202, f32[1536,4096]{1,0:T(8,128)} %get-tuple-element.143, bf16[1536,4096]{1,0:T(8,128)(2,1)} %add_convert_fusion.1), kind=kOutput, calls=%fused_computation.75 | convolution fusion | flops 12907970560 | bytes 74448896 | tf_op jit(solution)/shard_map/dot_general | solution.py:20
  726.8 15.4 convolution_convert_fusion.6
  742.2 25.1 %fusion.31 = (f32[1024]{0:T(1024)S(1)}, f32[1536]{0:T(1024)S(1)}, f32[1024]{0:T(1024)S(1)}, f32[1536]{0:T(1024)S(1)}, f32[1024]{0:T(1024)S(1)}, /*index=5*/f32[1024]{0:T(1024)S(1)}, bf16[1536,1024]{1,0:T(8,128)(2,1)}) fusion(f32[1536,1024]{1,0:T(8,128)} %copy-done.6, f32[1024]{0:T(1024)S(1)} %copy-done.47, f32[1024]{0:T(1024)S(1)} %copy-done.51, ...), kind=kOutput, calls=%fused_computation.91 | convolution fusion | flops 12925265920 | bytes 33591296 | tf_op jit(solution)/shard_map/dot_general | solution.py:20
  778.1 15.6 convolution_add_fusion.5
  796.7 22.2 %convolution_add_fusion.3 = f32[1024,4096]{1,0:T(8,128)} fusion(f32[1024,4096]{1,0:T(8,128)} %fusion.81, bf16[1536,1024]{1,0:T(8,128)(2,1)S(1)} %copy-done.19, bf16[1536,4096]{1,0:T(8,128)(2,1)} %get-tuple-element.83), kind=kOutput, calls=%fused_computation.77 | convolution fusion | flops 12889096192 | bytes 49283072 | tf_op jit(solution)/shard_map/dot_general | solution.py:20
  824.9 20.0 %convolution_convert_fusion = bf16[1536,4096]{1,0:T(8,128)(2,1)} fusion(bf16[1536,1024]{1,0:T(8,128)(2,1)} %bitcast.197, bf16[2048,1024]{1,0:T(8,128)(2,1)} %copy-done.29, bf16[2048,1024]{1,0:T(8,128)(2,1)} %param.27), kind=kOutput, calls=%fused_computation.58 | convolution fusion | flops 12907970560 | bytes 24117248 | tf_op jit(solution)/shard_map/dot_general | solution.py:20
  863.9 18.3 add_convert_fusion.2
  883.3 20.2 %add_convert_fusion = bf16[1536,4096]{1,0:T(8,128)(2,1)} fusion(bf16[1536,1024]{1,0:T(8,128)(2,1)S(1)} %add_convert_fusion.10, f32[4096]{0:T(1024)S(1)} %copy-done.80, bf16[1024,2048]{1,0:T(8,128)(2,1)} %copy-done.28, bf16[1024,2048]{1,0:T(8,128)(2,1)} %param.25), kind=kOutput, calls=%fused_computation.41 | convolution fusion | flops 12914262016 | bytes 24133632 | tf_op jit(solution)/shard_map/dot_general | solution.py:20
  903.5 24.6 %fusion.17 = (bf16[1536,4096]{1,0:T(8,128)(2,1)}, f32[1536,4096]{1,0:T(8,128)}) fusion(bf16[1536,4096]{1,0:T(8,128)(2,1)} %add_convert_fusion, bf16[1536,4096]{1,0:T(8,128)(2,1)} %convolution_convert_fusion), kind=kLoop, calls=%fused_computation.38 | loop fusion | flops 75497472 | bytes 62914560 | tf_op jit(solution)/shard_map/convert_element_type | solution.py:295
  928.1 22.9 %fusion.65 = f32[1536,1024]{1,0:T(8,128)} fusion(f32[1536,4096]{1,0:T(8,128)} %get-tuple-element.139, bf16[1536,4096]{1,0:T(8,128)(2,1)} %add_convert_fusion, bf16[2048,1024]{1,0:T(8,128)(2,1)} %copy-done.29, bf16[2048,1024]{1,0:T(8,128)(2,1)} %param.27), kind=kOutput, calls=%fused_computation.285 | convolution fusion | flops 12920553472 | bytes 52428800 | tf_op jit(solution)/shard_map/dot_general | solution.py:20
  951.0 77.0 %attention.5 = (bf16[6,256,1024]{2,1,0:T(8,128)(2,1)S(1)}, bf16[6,256,3072]{2,1,0:T(8,128)(2,1)}) custom-call(bf16[6,256,3072]{2,1,0:T(8,128)(2,1)} %bitcast.241, bf16[6,256,1024]{2,1,0:T(8,128)(2,1)S(1)} %bitcast.167, f32[256,128]{1,0:T(8,128)S(1)} %copy.41.cos_ref, f32[256,128]{1,0:T(8,128)S(1)} %copy.42.sin_ref, ...), custom_call_target="tpu_custom_call" | custom-call | flops 38654705664 | bytes 25165824 | tf_op jit(solution)/shard_map/attention/pallas_call | solution.py:97
  1042.4 28.9 %convolution_add_fusion = f32[4096,1024]{1,0:T(8,128)} fusion(f32[4096,1024]{1,0:T(8,128)} %convolution_add_fusion.1, bf16[1536,1024]{1,0:T(8,128)(2,1)S(1)} %bitcast.199, f32[1536,4096]{1,0:T(8,128)} %get-tuple-element.139, bf16[1536,4096]{1,0:T(8,128)(2,1)} %add_convert_fusion), kind=kOutput, calls=%fused_computation.74 | convolution fusion | flops 12907970560 | bytes 74448896 | tf_op jit(solution)/shard_map/dot_general | solution.py:20
  1071.3 49.9 %collective-permute-done.11 = f32[8,1024,128]{2,1,0:T(8,128)} collective-permute-done((f32[8,1024,128]{2,1,0:T(8,128)}, f32[8,1024,128]{2,1,0:T(8,128)}, u32[]{:S(2)}, u32[]{:S(2)}) %collective-permute-start.11) | collective-permute-done | bytes 4194336 | tf_op jit(solution)/shard_map/ppermute | solution.py:197
  1121.2 15.4 convolution_convert_fusion.4
  1136.7 24.9 %fusion.34 = (f32[1024]{0:T(1024)S(1)}, f32[1536]{0:T(1024)S(1)}, f32[1024]{0:T(1024)S(1)}, f32[1536]{0:T(1024)S(1)}, f32[1024]{0:T(1024)S(1)}, /*index=5*/f32[1024]{0:T(1024)S(1)}, bf16[1536,1024]{1,0:T(8,128)(2,1)}) fusion(f32[1536,1024]{1,0:T(8,128)} %copy-done.5, f32[1024]{0:T(1024)S(1)} %copy-done.48, f32[1024]{0:T(1024)S(1)} %copy-done.52, ...), kind=kOutput, calls=%fused_computation.94 | convolution fusion | flops 12925265920 | bytes 33591296 | tf_op jit(solution)/shard_map/dot_general | solution.py:20
  1173.6 15.9 convolution_add_fusion.4
  1191.4 25.7 %convolution_add_fusion.2 = f32[1024,4096]{1,0:T(8,128)} fusion(f32[1024,4096]{1,0:T(8,128)} %convolution_add_fusion.3, bf16[1536,1024]{1,0:T(8,128)(2,1)S(1)} %copy-done.17, bf16[1536,4096]{1,0:T(8,128)(2,1)} %get-tuple-element.97), kind=kOutput, calls=%fused_computation.76 | convolution fusion | flops 12889096192 | bytes 49283072 | tf_op jit(solution)/shard_map/dot_general | solution.py:20
  1268.0 382.1 %psum.7 = f32[12288]{0:T(1024)S(1)} all-reduce(f32[12288]{0:T(1024)S(1)} %constant_dynamic-update-slice_fusion.20), channel_id=1, replica_groups=mesh['tp'=2,'dp'=8] {'tp','dp'}, use_global_device_ids=true, to_apply=%region_33.34 | all-reduce | flops 12288 | bytes 98304 | tf_op jit(solution)/shard_map/psum | solution.py:353
  1655.9 10.1 add_convert_fusion.8
  1673.9 101.8 %scatter_rows.2.refs_4_ = f32[25152,128]{1,0:T(8,128)} custom-call(s32[4,1,2048]{2,1,0:T(1,128)S(1)} %reshape_reshape.20.refs_0_, s32[4,1,2048]{2,1,0:T(1,128)S(1)} %reshape_reshape.21.refs_1_, s32[6,1,2048]{2,1,0:T(1,128)S(1)} %reshape_reshape.26.refs_2_, s32[6,1,2048]{2,1,0:T(1,128)S(1)} %reshape_reshape.27.refs_3_, f32[8192,128]{1,0:T(8,128)} %bitcast.39.refs_4_, ...), custom_call_target="tpu_custom_call" | custom-call | flops 122880000000 | bytes 41943040 | tf_op jit(solution)/shard_map/scatter_rows/pallas_call | solution.py:178
  1785.4 27.2 %collective-permute-done.12 = f32[8,1536,128]{2,1,0:T(8,128)} collective-permute-done((f32[8,1536,128]{2,1,0:T(8,128)}, f32[8,1536,128]{2,1,0:T(8,128)}, u32[]{:S(2)}, u32[]{:S(2)}) %collective-permute-start.12) | collective-permute-done | bytes 6291488 | tf_op jit(solution)/shard_map/ppermute | solution.py:197
  1812.6 72.9 %scatter_rows.3 = f32[25152,128]{1,0:T(8,128)} custom-call(s32[6,1,2048]{2,1,0:T(1,128)S(1)} %reshape_reshape.24.refs_0_, s32[6,1,2048]{2,1,0:T(1,128)S(1)} %reshape_reshape.25.refs_1_, f32[12288,128]{1,0:T(8,128)} %bitcast.37.refs_2_, f32[12288,128]{1,0:T(8,128)} %bitcast.38.refs_3_, f32[25152,128]{1,0:T(8,128)} %scatter_rows.2.refs_4_), custom_call_target="tpu_custom_call" | custom-call | flops 73728000000 | bytes 25165824 | tf_op jit(solution)/shard_map/scatter_rows/pallas_call | solution.py:178
  (472 shorter events, 320.0 us)
Async XLA Ops:
  7.2 208.5 %all-gather.8.cloned.1.call-start = ((), (), s32[]{:S(2)}) async-start(), calls=%async_computation.8 | async-start | bytes 2359296 | tf_op jit(solution)/shard_map/all_gather | solution.py:214
  8.2 29.1 %collective-permute-start.3 = (f32[64,1024]{1,0:T(8,128)S(1)}, f32[64,1024]{1,0:T(8,128)}, u32[]{:S(2)}, u32[]{:S(2)}) collective-permute-start(f32[64,1024]{1,0:T(8,128)S(1)} %dynamic-slice_convert_fusion.3), channel_id=1, source_target_pairs={{0,8},{8,0},{1,9},{9,1},{2,10},{10,2},{3,11},{11,3},{4,12},{12,4},... | collective-permute-start | bytes 786440 | tf_op jit(solution)/shard_map/ppermute | solution.py:197
  37.3 199.2 %all-gather.6.cloned.1.call-start = ((), (), s32[]{:S(2)}) async-start(), calls=%async_computation.7 | async-start | bytes 7077888 | tf_op jit(solution)/shard_map/all_gather | solution.py:214
  40.1 53.5 %copy-start.81 = (bf16[8,3,64]{2,0,1:T(8,128)(2,1)S(1)}, bf16[8,3,64]{2,0,1:T(8,128)(2,1)}, u32[]{:S(2)}) copy-start(bf16[8,3,64]{2,0,1:T(8,128)(2,1)} %param.22) | copy-start | bytes 9220
  40.1 53.6 %copy-start.86 = (bf16[2048]{0:T(1024)(128)(2,1)S(1)}, bf16[2048]{0:T(1024)(128)(2,1)}, u32[]{:S(2)}) copy-start(bf16[2048]{0:T(1024)(128)(2,1)} %param.26) | copy-start | bytes 12292
  40.1 54.2 %copy-start.44 = (s32[32,256]{1,0:T(8,128)S(1)}, s32[32,256]{1,0:T(8,128)}, u32[]{:S(2)}) copy-start(s32[32,256]{1,0:T(8,128)} %param.15) | copy-start | bytes 98308
  44.5 19.1 %collective-permute-start.1 = (f32[384,512]{0,1:T(8,128)S(1)}, f32[384,512]{0,1:T(8,128)}, u32[]{:S(2)}, u32[]{:S(2)}) collective-permute-start(f32[384,512]{0,1:T(8,128)S(1)} %dynamic-slice_convert_fusion.2), channel_id=1, source_target_pairs={{0,8},{8,0},{1,9},{9,1},{2,10},{10,2},{3,11},{11,3},{4,12},{12,4},... | collective-permute-start | bytes 2359304 | tf_op jit(solution)/shard_map/ppermute | solution.py:197
  63.7 253.0 %all-gather.10.cloned.1.call-start = ((), (), s32[]{:S(2)}) async-start(), calls=%async_computation.9 | async-start | bytes 9437184 | tf_op jit(solution)/shard_map/all_gather | solution.py:214
  64.9 23.9 %collective-permute-start.4 = (f32[256,1024]{1,0:T(8,128)S(1)}, f32[256,1024]{1,0:T(8,128)}, u32[]{:S(2)}, u32[]{:S(2)}) collective-permute-start(f32[256,1024]{1,0:T(8,128)S(1)} %dynamic-slice_convert_fusion.1), channel_id=1, source_target_pairs={{0,8},{8,0},{1,9},{9,1},{2,10},{10,2},{3,11},{11,3},{4,12},{12,4},... | collective-permute-start | bytes 3145736 | tf_op jit(solution)/shard_map/ppermute | solution.py:197
  88.9 248.3 %all-gather.12.cloned.1.call-start = ((), (), s32[]{:S(2)}) async-start(), calls=%async_computation.10 | async-start | bytes 9437184 | tf_op jit(solution)/shard_map/all_gather | solution.py:214
  89.4 132.9 %collective-permute-start = (f32[1024,1024]{1,0:T(8,128)}, f32[1024,1024]{1,0:T(8,128)}, u32[]{:S(2)}, u32[]{:S(2)}) collective-permute-start(f32[1024,1024]{1,0:T(8,128)} %select_convert_fusion.2), channel_id=1, source_target_pairs={{0,8},{8,0},{1,9},{9,1},{2,10},{10,2},{3,11},{11,3},{4,12},{12,4},... | collective-permute-start | bytes 12582920 | tf_op jit(solution)/shard_map/ppermute | solution.py:197
  92.1 113.5 %collective-permute-start.5 = (f32[128,2048]{1,0:T(8,128)}, f32[128,2048]{1,0:T(8,128)}, u32[]{:S(2)}, u32[]{:S(2)}) collective-permute-start(f32[128,2048]{1,0:T(8,128)} %dynamic-slice_convert_fusion), channel_id=1, source_target_pairs={{0,8},{8,0},{1,9},{9,1},{2,10},{10,2},{3,11},{11,3},{4,12},{12,4},... | collective-permute-start | bytes 3145736 | tf_op jit(solution)/shard_map/ppermute | solution.py:197
  93.6 121.9 %collective-permute-start.2 = (f32[3584]{0:T(1024)S(1)}, f32[3584]{0:T(1024)S(1)}, u32[]{:S(2)}, u32[]{:S(2)}) collective-permute-start(f32[3584]{0:T(1024)S(1)} %maximum_convert_fusion), channel_id=1, source_target_pairs={{0,8},{8,0},{1,9},{9,1},{2,10},{10,2},{3,11},{11,3},{4,12},{12,4},... | collective-permute-start | bytes 43016 | tf_op jit(solution)/shard_map/ppermute | solution.py:197
  111.7 362.8 %collective-permute-start.7 = (f32[1536,1024]{1,0:T(8,128)}, f32[1536,1024]{1,0:T(8,128)}, u32[]{:S(2)}, u32[]{:S(2)}) collective-permute-start(f32[1536,1024]{1,0:T(8,128)} %select_convert_fusion.1), channel_id=1, source_target_pairs={{0,8},{8,0},{1,9},{9,1},{2,10},{10,2},{3,11},{11,3},{4,12},{12,4},... | collective-permute-start | bytes 18874376 | tf_op jit(solution)/shard_map/ppermute | solution.py:197
  130.6 688.4 %collective-permute-start.9 = (f32[1536,1024]{1,0:T(8,128)}, f32[1536,1024]{1,0:T(8,128)}, u32[]{:S(2)}, u32[]{:S(2)}) collective-permute-start(f32[1536,1024]{1,0:T(8,128)} %select_convert_fusion), channel_id=1, source_target_pairs={{0,8},{8,0},{1,9},{9,1},{2,10},{10,2},{3,11},{11,3},{4,12},{12,4},... | collective-permute-start | bytes 18874376 | tf_op jit(solution)/shard_map/ppermute | solution.py:197
  215.6 126.3 %copy-start.78 = (f32[4096]{0:T(1024)}, f32[4096]{0:T(1024)S(1)}, u32[]{:S(2)}) copy-start(f32[4096]{0:T(1024)S(1)} %pad_maximum_fusion.4) | copy-start | bytes 49156
  215.7 29.9 %copy-start.94 = (f32[3072]{0:T(1024)}, f32[3072]{0:T(1024)S(1)}, u32[]{:S(2)}) copy-start(f32[3072]{0:T(1024)S(1)} %constant_dynamic-update-slice_fusion.12) | copy-start | bytes 36868
  257.2 55.1 %copy-start.25 = (bf16[4,256,1024]{2,1,0:T(8,128)(2,1)S(1)}, bf16[4,256,1024]{2,1,0:T(8,128)(2,1)}, u32[]{:S(2)}) copy-start(bf16[4,256,1024]{2,1,0:T(8,128)(2,1)} %get-tuple-element.147) | copy-start | bytes 6291460
  412.7 33.6 %slice-start = ((s8[6291456]{0:T(1024)(128)(4,1)}), s8[4194304]{0:T(1024)(128)(4,1)S(1)}, s32[]{:S(2)}) async-start(s8[6291456]{0:T(1024)(128)(4,1)} %bitcast.163), calls=%async_computation.15 | async-start | bytes 8388608
  423.5 22.8 %slice-start.1 = ((s8[6291456]{0:T(1024)(128)(4,1)}), s8[2097152]{0:T(1024)(128)(4,1)S(1)}, s32[]{:S(2)}) async-start(s8[6291456]{0:T(1024)(128)(4,1)} %bitcast.163), calls=%async_computation.16 | async-start | bytes 4194304
  499.4 227.3 %all-to-all-start = ((f32[8,1024,128]{2,1,0:T(8,128)}), f32[8,1024,128]{2,1,0:T(8,128)}, u32[]{:S(2)}, u32[]{:S(2)}) async-start(f32[8,1024,128]{2,1,0:T(8,128)} %bitcast_bitcast_fusion.2), calls=%async_computation | async-start | bytes 8388608 | tf_op jit(solution)/shard_map/all_to_all | solution.py:308
  504.3 567.0 %collective-permute-start.6 = (f32[1024,1024]{1,0:T(8,128)}, f32[1024,1024]{1,0:T(8,128)}, u32[]{:S(2)}, u32[]{:S(2)}) collective-permute-start(f32[1024,1024]{1,0:T(8,128)} %add_add_fusion.2), channel_id=1, source_target_pairs={{0,8},{8,0},{1,9},{9,1},{2,10},{10,2},{3,11},{11,3},{4,12},{12,4},... | collective-permute-start | bytes 12582920 | tf_op jit(solution)/shard_map/ppermute | solution.py:197
  518.3 100.4 %copy-start.6 = (f32[1536,1024]{1,0:T(8,128)}, f32[1536,1024]{1,0:T(8,128)S(1)}, u32[]{:S(2)}) copy-start(f32[1536,1024]{1,0:T(8,128)S(1)} %get-tuple-element.145) | copy-start | bytes 18874372
  536.5 77.1 %copy-start.23 = (bf16[6,256,1024]{2,1,0:T(8,128)(2,1)S(1)}, bf16[6,256,1024]{2,1,0:T(8,128)(2,1)}, u32[]{:S(2)}) copy-start(bf16[6,256,1024]{2,1,0:T(8,128)(2,1)} %get-tuple-element.153) | copy-start | bytes 9437188
  536.5 77.1 %copy-start.98 = (f32[1024,1024]{1,0:T(8,128)S(1)}, f32[1024,1024]{1,0:T(8,128)}, u32[]{:S(2)}) copy-start(f32[1024,1024]{1,0:T(8,128)} %convolution_bitcast_fusion) | copy-start | bytes 12582916
  742.2 25.1 %copy-start.24 = (bf16[6,256,1024]{2,1,0:T(8,128)(2,1)S(1)}, bf16[6,256,1024]{2,1,0:T(8,128)(2,1)}, u32[]{:S(2)}) copy-start(bf16[6,256,1024]{2,1,0:T(8,128)(2,1)} %get-tuple-element.153) | copy-start | bytes 9437188
  742.2 25.1 %copy-start.56 = (f32[1536]{0:T(1024)S(1)}, f32[1536]{0:T(1024)}, u32[]{:S(2)}) copy-start(f32[1536]{0:T(1024)} %copy-done.55) | copy-start | bytes 18436
  845.0 276.2 %all-to-all-start.1 = ((f32[8,1536,128]{2,1,0:T(8,128)}), f32[8,1536,128]{2,1,0:T(8,128)}, u32[]{:S(2)}, u32[]{:S(2)}) async-start(f32[8,1536,128]{2,1,0:T(8,128)} %bitcast.188), calls=%async_computation.1 | async-start | bytes 12582912 | tf_op jit(solution)/shard_map/all_to_all | solution.py:308
  849.9 802.1 %reduce-scatter.9.cloned.1.call-start = ((), (), s32[]{:S(2)}) async-start(), calls=%async_computation.13 | async-start | bytes 4718592 | tf_op jit(solution)/shard_map/reduce_scatter | solution.py:337
  951.0 78.3 %copy-start.8 = (bf16[1536,1024]{1,0:T(8,128)(2,1)S(1)}, bf16[1536,1024]{1,0:T(8,128)(2,1)}, u32[]{:S(2)}) copy-start(bf16[1536,1024]{1,0:T(8,128)(2,1)} %gather_fusion.3) | copy-start | bytes 9437188
  951.0 78.3 %copy-start.40 = (bf16[512,1024]{1,0:T(8,128)(2,1)S(1)}, bf16[512,1024]{1,0:T(8,128)(2,1)}, u32[]{:S(2)}) copy-start(bf16[512,1024]{1,0:T(8,128)(2,1)} %copy-done.37) | copy-start | bytes 3145732
  951.0 78.3 %copy-start.77 = (bf16[8,64,1024]{2,1,0:T(8,128)(2,1)S(1)}, bf16[8,64,1024]{2,1,0:T(8,128)(2,1)}, u32[]{:S(2)}) copy-start(bf16[8,64,1024]{2,1,0:T(8,128)(2,1)} %param.23) | copy-start | bytes 3145732
  951.0 78.3 %copy-start.97 = (f32[1536,1024]{1,0:T(8,128)S(1)}, f32[1536,1024]{1,0:T(8,128)}, u32[]{:S(2)}) copy-start(f32[1536,1024]{1,0:T(8,128)} %fusion.65) | copy-start | bytes 18874372
  1028.0 93.2 %collective-permute-start.11 = (f32[8,1024,128]{2,1,0:T(8,128)}, f32[8,1024,128]{2,1,0:T(8,128)}, u32[]{:S(2)}, u32[]{:S(2)}) collective-permute-start(f32[8,1024,128]{2,1,0:T(8,128)} %all-to-all-done), channel_id=1, source_target_pairs={{0,8},{8,0},{1,9},{9,1},{2,10},{10,2},{3,11},{11,3},{4,12},{12,4},... | collective-permute-start | bytes 12582920 | tf_op jit(solution)/shard_map/ppermute | solution.py:197
  1042.4 733.4 %reduce-scatter.5.cloned.1.call-start = ((), (), s32[]{:S(2)}) async-start(), calls=%async_computation.11 | async-start | bytes 14155776 | tf_op jit(solution)/shard_map/reduce_scatter | solution.py:337
  1136.7 25.0 %copy-start.54 = (f32[1536]{0:T(1024)S(1)}, f32[1536]{0:T(1024)}, u32[]{:S(2)}) copy-start(f32[1536]{0:T(1024)} %copy-done.53) | copy-start | bytes 18436
  1189.5 590.2 %reduce-scatter.7.cloned.1.call-start = ((), (), s32[]{:S(2)}) async-start(), calls=%async_computation.12 | async-start | bytes 18874368 | tf_op jit(solution)/shard_map/reduce_scatter | solution.py:337
  1190.3 591.8 %reduce-scatter.11.cloned.1.call-start = ((), (), s32[]{:S(2)}) async-start(), calls=%async_computation.14 | async-start | bytes 18874368 | tf_op jit(solution)/shard_map/reduce_scatter | solution.py:337
  1218.4 437.5 %collective-permute-start.8 = (f32[1536,1024]{1,0:T(8,128)}, f32[1536,1024]{1,0:T(8,128)}, u32[]{:S(2)}, u32[]{:S(2)}) collective-permute-start(f32[1536,1024]{1,0:T(8,128)} %add_add_fusion.1), channel_id=1, source_target_pairs={{0,8},{8,0},{1,9},{9,1},{2,10},{10,2},{3,11},{11,3},{4,12},{12,4},... | collective-permute-start | bytes 18874376 | tf_op jit(solution)/shard_map/ppermute | solution.py:197
  1219.2 436.7 %collective-permute-start.10 = (f32[1536,1024]{1,0:T(8,128)}, f32[1536,1024]{1,0:T(8,128)}, u32[]{:S(2)}, u32[]{:S(2)}) collective-permute-start(f32[1536,1024]{1,0:T(8,128)} %add_add_fusion), channel_id=1, source_target_pairs={{0,8},{8,0},{1,9},{9,1},{2,10},{10,2},{3,11},{11,3},{4,12},{12,4},... | collective-permute-start | bytes 18874376 | tf_op jit(solution)/shard_map/ppermute | solution.py:197
  1247.6 426.3 %all-to-all-start.2 = ((f32[8,1536,128]{2,1,0:T(8,128)}), f32[8,1536,128]{2,1,0:T(8,128)}, u32[]{:S(2)}, u32[]{:S(2)}) async-start(f32[8,1536,128]{2,1,0:T(8,128)} %bitcast.187), calls=%async_computation.2 | async-start | bytes 12582912 | tf_op jit(solution)/shard_map/all_to_all | solution.py:308
  1252.8 421.1 %collective-permute-start.13 = (f32[8,1536,128]{2,1,0:T(8,128)}, f32[8,1536,128]{2,1,0:T(8,128)}, u32[]{:S(2)}, u32[]{:S(2)}) collective-permute-start(f32[8,1536,128]{2,1,0:T(8,128)} %all-to-all-done.1), channel_id=1, source_target_pairs={{0,8},{8,0},{1,9},{9,1},{2,10},{10,2},{3,11},{11,3},{4,12},{12,4},... | collective-permute-start | bytes 18874376 | tf_op jit(solution)/shard_map/ppermute | solution.py:197
  1653.7 231.8 %collective-permute-start.15 = (f32[512,128]{1,0:T(8,128)}, f32[512,128]{1,0:T(8,128)}, u32[]{:S(2)}, u32[]{:S(2)}) collective-permute-start(f32[512,128]{1,0:T(8,128)} %slice.204), channel_id=1, source_target_pairs={{0,8},{8,0},{1,9},{9,1},{2,10},{10,2},{3,11},{11,3},{4,12},{12,4},... | collective-permute-start | bytes 786440 | tf_op jit(solution)/shard_map/ppermute | solution.py:197
  1673.9 138.7 %collective-permute-start.12 = (f32[8,1536,128]{2,1,0:T(8,128)}, f32[8,1536,128]{2,1,0:T(8,128)}, u32[]{:S(2)}, u32[]{:S(2)}) collective-permute-start(f32[8,1536,128]{2,1,0:T(8,128)} %all-to-all-done.2), channel_id=1, source_target_pairs={{0,8},{8,0},{1,9},{9,1},{2,10},{10,2},{3,11},{11,3},{4,12},{12,4},... | collective-permute-start | bytes 18874376 | tf_op jit(solution)/shard_map/ppermute | solution.py:197
  1777.7 107.8 %collective-permute-start.17 = (f32[128,1536]{0,1:T(8,128)S(1)}, f32[128,1536]{0,1:T(8,128)}, u32[]{:S(2)}, u32[]{:S(2)}) collective-permute-start(f32[128,1536]{0,1:T(8,128)S(1)} %bitcast.220), channel_id=1, source_target_pairs={{0,8},{8,0},{1,9},{9,1},{2,10},{10,2},{3,11},{11,3},{4,12},{12,4},... | collective-permute-start | bytes 2359304 | tf_op jit(solution)/shard_map/ppermute | solution.py:197
  1782.0 103.5 %collective-permute-start.14 = (f32[2048,128]{1,0:T(8,128)}, f32[2048,128]{1,0:T(8,128)S(1)}, u32[]{:S(2)}, u32[]{:S(2)}) collective-permute-start(f32[2048,128]{1,0:T(8,128)} %slice.203), channel_id=1, source_target_pairs={{0,8},{8,0},{1,9},{9,1},{2,10},{10,2},{3,11},{11,3},{4,12},{12,4},... | collective-permute-start | bytes 3145736 | tf_op jit(solution)/shard_map/ppermute | solution.py:197
  1783.4 102.2 %collective-permute-start.16 = (f32[128,2048]{1,0:T(8,128)S(1)}, f32[128,2048]{1,0:T(8,128)S(1)}, u32[]{:S(2)}, u32[]{:S(2)}) collective-permute-start(f32[128,2048]{1,0:T(8,128)S(1)} %slice.205), channel_id=1, source_target_pairs={{0,8},{8,0},{1,9},{9,1},{2,10},{10,2},{3,11},{11,3},{4,12},{12,4},... | collective-permute-start | bytes 3145736 | tf_op jit(solution)/shard_map/ppermute | solution.py:197
  1812.6 75.3 %copy-start.34 = (f32[4096,128]{1,0:T(8,128)S(1)}, f32[4096,128]{1,0:T(8,128)}, u32[]{:S(2)}) copy-start(f32[4096,128]{1,0:T(8,128)} %reduce-scatter.7.cloned.1.call-done) | copy-start | bytes 6291460
  (93 other events, 887.8 us)
Sparse Core Ops, SparseCore 0:
  37.4 24.0 all-gather.7
  63.8 41.5 all-gather.5
  107.3 51.5 all-gather.9
  205.8 50.5 all-gather.11
  1042.5 46.0 reduce-scatter.8
  1189.6 121.3 reduce-scatter.4
  1314.6 109.4 reduce-scatter.6
  1427.6 110.5 reduce-scatter.10
